TPU v7x, 32 devices: a whole 2x2x4 slice. The times are simulated.
32 devices in a mesh: row: 4 (over x, core), col: 8 (over z, y).
Axes of the slice: x: 2, y: 2, z: 4, core: 2. Of those that a mesh axis runs over, the one named last changes fastest.
Arguments:
- inputs: bfloat16 [512, 6144], P('col', 'row'), may hold values from -6 to 6
- cotangent: bfloat16 [512, 6144], P('col', 'row'), may hold values from -6 to 6
- weight_in: bfloat16 [6144, 12288], P('row', 'col'), may hold values from -0.078125 to 0.078125
- moment_in: bfloat16 [6144, 12288], P('row', 'col'), may hold values from -5 to 5
- second_in: bfloat16 [6144, 12288], P('row', 'col'), may hold values from 0.049804688 to 2
- weight_out: bfloat16 [12288, 6144], P('col', 'row'), may hold values from -0.0546875 to 0.0546875
- moment_out: bfloat16 [12288, 6144], P('col', 'row'), may hold values from -5 to 5
- second_out: bfloat16 [12288, 6144], P('col', 'row'), may hold values from 0.049804688 to 2
Outputs:
- input_grad: bfloat16 [512, 6144], P('col', 'row')
- update_in: bfloat16 [6144, 12288], P('row', 'col')
- code_moment_in: bfloat16 [6144, 12288], P('row', 'col')
- code_second_in: bfloat16 [6144, 12288], P('row', 'col')
- row_scale_in: float32 [2, 6144], P(None, 'row')
- col_scale_in: float32 [2, 12288], P(None, 'col')
- update_out: bfloat16 [12288, 6144], P('col', 'row')
- code_moment_out: bfloat16 [12288, 6144], P('col', 'row')
- code_second_out: bfloat16 [12288, 6144], P('col', 'row')
- row_scale_out: float32 [2, 12288], P(None, 'col')
- col_scale_out: float32 [2, 6144], P(None, 'row')
All inputs are finite; a program needn't handle non-finite values. Where the computation divides by a largest or mean magnitude, that divisor is 1e-20 or more.
Results may differ from a plain program's by a relative error of at most 0.0049.
Values may be sent and summed in bfloat16 or wider, within the bound.
A program may use at most 192 MiB of HBM per device.

v0:
```python
import functools

import jax
import jax.numpy as jnp
from jax import lax
from jax.experimental import pallas as pl
from jax.experimental.pallas import tpu as pltpu
from jax.sharding import PartitionSpec as P

root_half = 0.7071067811865476
normal_density = 0.3989422804014327
momentum_decay = 0.9
second_decay = 0.95
stable_eps = 1e-08
weight_decay = 0.1
LANES = 128


def contract(left, right, left_dim, right_dim):
    return lax.dot_general(
        left, right, (((left_dim,), (right_dim,)), ((), ())), preferred_element_type=jnp.float32
    )


def activate(preact, hidden_grad):
    cumulative = 0.5 * (1.0 + lax.erf(preact * root_half))
    density = jnp.exp(-0.5 * preact * preact) * normal_density
    hidden = (preact * cumulative).astype(jnp.bfloat16)
    delta = (hidden_grad * (cumulative + preact * density)).astype(jnp.bfloat16)
    return (hidden, delta)


def exchange_kernel(plan, sizes, *refs):
    count = len(plan)
    sources, targets = refs[:count], refs[count : 2 * count]
    send_sem, recv_sem, own_sem = refs[2 * count :]
    axes = sorted(set(axis for axis, _ in plan))
    me = {axis: lax.axis_index(axis) for axis in axes}
    barrier = pltpu.get_barrier_semaphore()
    greeted = 0
    for axis in axes:
        for step in range(1, sizes[axis]):
            peer = lax.rem(me[axis] + step, sizes[axis])
            pl.semaphore_signal(
                barrier, inc=1, device_id={axis: peer}, device_id_type=pl.DeviceIdType.MESH
            )
            greeted += 1
    owns = []
    for item, (axis, scatter) in enumerate(plan):
        block = sources[item].at[me[axis]] if scatter else sources[item]
        own = pltpu.make_async_copy(block, targets[item].at[me[axis]], own_sem.at[item])
        own.start()
        owns.append(own)
    pl.semaphore_wait(barrier, greeted)
    copies = []
    at = 0
    for item, (axis, scatter) in enumerate(plan):
        for step in range(1, sizes[axis]):
            peer = lax.rem(me[axis] + step, sizes[axis])
            block = sources[item].at[peer] if scatter else sources[item]
            copy = pltpu.make_async_remote_copy(
                src_ref=block,
                dst_ref=targets[item].at[me[axis]],
                send_sem=send_sem.at[at],
                recv_sem=recv_sem.at[at],
                device_id={axis: peer},
                device_id_type=pl.DeviceIdType.MESH,
            )
            copy.start()
            copies.append(copy)
            at += 1
    for own in owns:
        own.wait()
    for copy in copies:
        copy.wait()


def exchange(identity, plan, sizes, *arrays):
    flights = sum(sizes[axis] - 1 for axis, _ in plan)
    shapes = [
        jax.ShapeDtypeStruct(
            array.shape if scatter else (sizes[axis],) + array.shape, array.dtype
        )
        for array, (axis, scatter) in zip(arrays, plan)
    ]
    return pl.pallas_call(
        functools.partial(exchange_kernel, plan, sizes),
        out_shape=shapes,
        in_specs=[pl.BlockSpec(memory_space=pl.ANY)] * len(plan),
        out_specs=[pl.BlockSpec(memory_space=pl.ANY)] * len(plan),
        scratch_shapes=[
            pltpu.SemaphoreType.DMA((flights,)),
            pltpu.SemaphoreType.DMA((flights,)),
            pltpu.SemaphoreType.DMA((len(plan),)),
        ],
        compiler_params=pltpu.CompilerParams(collective_id=identity, has_side_effects=True),
        name=f"exchange{identity}",
    )(*arrays)


def lane_fold(values, combine):
    folded = values[:, :LANES]
    for at in range(LANES, values.shape[1], LANES):
        folded = combine(folded, values[:, at : at + LANES])
    return folded


def squares_kernel(left_ref, right_ref, total_ref):
    gradient = contract(left_ref[...], right_ref[...], 0, 0)
    folded = lane_fold(gradient * gradient, jnp.add)
    folded = jnp.sum(folded.reshape(-1, 8, LANES), axis=0)

    @pl.when(pl.program_id(0) == 0)
    def _():
        total_ref[...] = jnp.zeros_like(total_ref)

    total_ref[...] += folded


def row_block(rows):
    return 256 if rows % 256 == 0 else 128


def squares(left, right):
    tokens, rows = left.shape
    block = row_block(rows)
    return pl.pallas_call(
        squares_kernel,
        grid=(rows // block,),
        out_shape=jax.ShapeDtypeStruct((8, LANES), jnp.float32),
        in_specs=[
            pl.BlockSpec((tokens, block), lambda i: (0, i)),
            pl.BlockSpec(right.shape, lambda i: (0, 0)),
        ],
        out_specs=pl.BlockSpec((8, LANES), lambda i: (0, 0)),
        name="squares",
    )(left, right)


def to_lanes(column_tops):
    pieces = []
    for at in range(0, column_tops.shape[0], LANES):
        turned = column_tops[at : at + LANES].T
        pieces.append(jnp.max(turned, axis=0, keepdims=True))
    return jnp.concatenate(pieces, axis=1)


def moments_kernel(
    factor_ref, left_ref, right_ref, weight_ref, moment_ref, second_ref,
    update_ref, new_moment_ref, new_second_ref, row_ref, col_ref,
):
    gradient = contract(left_ref[...], right_ref[...], 0, 0)
    scaled = gradient * factor_ref[0, 0]
    moment_new = momentum_decay * moment_ref[...].astype(jnp.float32) + (
        1.0 - momentum_decay
    ) * scaled
    second_new = second_decay * second_ref[...].astype(jnp.float32) + (
        1.0 - second_decay
    ) * scaled * scaled
    update = moment_new / (jnp.sqrt(second_new) + stable_eps) + weight_decay * weight_ref[
        ...
    ].astype(jnp.float32)
    update_ref[...] = update.astype(jnp.bfloat16)
    new_moment_ref[...] = moment_new.astype(jnp.bfloat16)
    new_second_ref[...] = second_new.astype(jnp.bfloat16)
    size = jnp.abs(moment_new)
    row_ref[0:1, :] = to_lanes(lane_fold(size, jnp.maximum))
    row_ref[1:2, :] = to_lanes(lane_fold(second_new, jnp.maximum))

    @pl.when(pl.program_id(0) == 0)
    def _():
        col_ref[...] = jnp.zeros_like(col_ref)

    col_ref[0:1, :] = jnp.maximum(col_ref[0:1, :], jnp.max(size, axis=0, keepdims=True))
    col_ref[1:2, :] = jnp.maximum(col_ref[1:2, :], jnp.max(second_new, axis=0, keepdims=True))


def moments(factor, left, right, weight, moment, second):
    rows, cols = weight.shape
    tokens = left.shape[0]
    block = row_block(rows)
    tile = pl.BlockSpec((block, cols), lambda i: (i, 0))
    half = jax.ShapeDtypeStruct((rows, cols), jnp.bfloat16)
    return pl.pallas_call(
        moments_kernel,
        grid=(rows // block,),
        out_shape=[
            half,
            half,
            half,
            jax.ShapeDtypeStruct((2, rows), jnp.float32),
            jax.ShapeDtypeStruct((2, cols), jnp.float32),
        ],
        in_specs=[
            pl.BlockSpec(memory_space=pltpu.SMEM),
            pl.BlockSpec((tokens, block), lambda i: (0, i)),
            pl.BlockSpec((tokens, cols), lambda i: (0, 0)),
            tile,
            tile,
            tile,
        ],
        out_specs=[
            tile,
            tile,
            tile,
            pl.BlockSpec((2, block), lambda i: (0, i)),
            pl.BlockSpec((2, cols), lambda i: (0, 0)),
        ],
        name="moments",
    )(factor, left, right, weight, moment, second)


def encode_kernel(moment_ref, second_ref, row_ref, col_ref, code_moment_ref, code_second_ref):
    rows, cols = moment_ref.shape
    for which, (source, target) in enumerate(
        ((moment_ref, code_moment_ref), (second_ref, code_second_ref))
    ):
        for low in range(0, rows, LANES):
            span = pl.ds(low, LANES)
            inverse = 1.0 / row_ref[which : which + 1, low : low + LANES]
            inverse = jnp.broadcast_to(inverse, (LANES, LANES)).T
            for at in range(0, cols, LANES):
                other = 1.0 / col_ref[which : which + 1, at : at + LANES]
                value = source[span, at : at + LANES].astype(jnp.float32)
                target[span, at : at + LANES] = (value * jnp.maximum(inverse, other)).astype(
                    jnp.bfloat16
                )


def encode(moment, second, row_top, col_top):
    rows, cols = moment.shape
    block = row_block(rows)
    tile = pl.BlockSpec((block, cols), lambda i: (i, 0))
    half = jax.ShapeDtypeStruct((rows, cols), jnp.bfloat16)
    return pl.pallas_call(
        encode_kernel,
        grid=(rows // block,),
        out_shape=[half, half],
        in_specs=[
            tile,
            tile,
            pl.BlockSpec((2, block), lambda i: (0, i)),
            pl.BlockSpec((2, cols), lambda i: (0, 0)),
        ],
        out_specs=[tile, tile],
        name="encode",
    )(moment, second, row_top, col_top)


def shards(
    sizes, inputs, cotangent, weight_in, moment_in, second_in, weight_out, moment_out, second_out
):
    rows, cols = sizes["row"], sizes["col"]
    width_in, hidden_cols = weight_in.shape
    width = inputs.shape[1]
    tokens = inputs.shape[0] * cols
    entries = 2.0 * width_in * rows * hidden_cols * cols
    all_inputs, all_cotangent = exchange(
        0, (("col", False), ("col", False)), sizes, inputs, cotangent
    )
    all_inputs = all_inputs.reshape(tokens, width)
    all_cotangent = all_cotangent.reshape(tokens, width)
    preact_part = contract(all_inputs, weight_in, 1, 0).astype(jnp.bfloat16)
    grad_part = contract(all_cotangent, weight_out, 1, 1).astype(jnp.bfloat16)
    parts = (rows, tokens // rows, hidden_cols)
    preact_parts, grad_parts = exchange(
        1,
        (("row", True), ("row", True)),
        sizes,
        preact_part.reshape(parts),
        grad_part.reshape(parts),
    )
    preact = jnp.sum(preact_parts.astype(jnp.float32), axis=0)
    hidden_grad = jnp.sum(grad_parts.astype(jnp.float32), axis=0)
    hidden, delta = activate(preact, hidden_grad)
    all_hidden, all_delta = exchange(2, (("row", False), ("row", False)), sizes, hidden, delta)
    all_hidden = all_hidden.reshape(tokens, hidden_cols)
    all_delta = all_delta.reshape(tokens, hidden_cols)
    grad_input_part = contract(all_delta, weight_in, 1, 1).astype(jnp.bfloat16)
    local_total = squares(all_inputs, all_delta) + squares(all_hidden, all_cotangent)
    grad_input_parts, totals = exchange(
        3,
        (("col", True), ("col", False)),
        sizes,
        grad_input_part.reshape(cols, tokens // cols, width),
        local_total,
    )
    input_grad = jnp.sum(grad_input_parts.astype(jnp.float32), axis=0).astype(jnp.bfloat16)
    (totals,) = exchange(4, (("row", False),), sizes, jnp.sum(totals, axis=0))
    total = jnp.sum(totals)
    factor = 1.0 / jnp.maximum(jnp.sqrt(total / entries), 1.0)
    factor = factor.reshape(1, 1)
    update_in, moment_new_in, second_new_in, rows_in, cols_in = moments(
        factor, all_inputs, all_delta, weight_in, moment_in, second_in
    )
    update_out, moment_new_out, second_new_out, rows_out, cols_out = moments(
        factor, all_hidden, all_cotangent, weight_out, moment_out, second_out
    )
    rows_in, cols_out, cols_in, rows_out = exchange(
        5,
        (("col", False), ("col", False), ("row", False), ("row", False)),
        sizes,
        rows_in,
        cols_out,
        cols_in,
        rows_out,
    )
    rows_in, cols_out, cols_in, rows_out = (
        jnp.maximum(jnp.max(tops, axis=0), 1.0) for tops in (rows_in, cols_out, cols_in, rows_out)
    )
    code_moment_in, code_second_in = encode(moment_new_in, second_new_in, rows_in, cols_in)
    code_moment_out, code_second_out = encode(moment_new_out, second_new_out, rows_out, cols_out)
    return (
        input_grad,
        update_in,
        code_moment_in,
        code_second_in,
        rows_in,
        cols_in,
        update_out,
        code_moment_out,
        code_second_out,
        rows_out,
        cols_out,
    )


def solution(mesh):
    in_specs = (
        P("col", "row"),
        P("col", "row"),
        P("row", "col"),
        P("row", "col"),
        P("row", "col"),
        P("col", "row"),
        P("col", "row"),
        P("col", "row"),
    )
    out_specs = (
        P("col", "row"),
        P("row", "col"),
        P("row", "col"),
        P("row", "col"),
        P(None, "row"),
        P(None, "col"),
        P("col", "row"),
        P("col", "row"),
        P("col", "row"),
        P(None, "col"),
        P(None, "row"),
    )
    sizes = {axis: mesh.shape[axis] for axis in ("row", "col")}
    return jax.shard_map(
        functools.partial(shards, sizes),
        mesh=mesh,
        in_specs=in_specs,
        out_specs=out_specs,
        check_vma=False,
    )
```

profile of v0, /device:TPU:0, one launch (start us, length us, event | category | flops | bytes accessed | tf_op | source)
XLA Modules:
  0.0 298.3 jit_solution(17208676402667381505)
XLA Ops:
  0.6 0.0 slice-start
  0.7 62.7 %exchange0.1 = (bf16[8,64,1536]{2,1,0:T(8,128)(2,1)}, bf16[8,64,1536]{2,1,0:T(8,128)(2,1)}) custom-call(bf16[64,1536]{1,0:T(8,128)(2,1)} %refs_0_.1, bf16[64,1536]{1,0:T(8,128)(2,1)} %refs_1_.1), custom_call_target="tpu_custom_call" | custom-call | tf_op jit(solution)/shard_map/exchange0/pallas_call | solution.py:86
  63.4 0.0 copy-start
  63.4 0.0 slice-start.1
  63.4 6.7 %convolution_convert_fusion.1 = bf16[512,1536]{1,0:T(8,128)(2,1)} fusion(bf16[512,1536]{1,0:T(8,128)(2,1)} %bitcast.17, bf16[1536,1536]{1,0:T(8,128)(2,1)} %weight_ref.3), kind=kOutput, calls=%fused_computation.3 | convolution fusion | flops 2416705536 | bytes 7864320 | tf_op jit(solution)/shard_map/dot_general | solution.py:20
  70.1 0.0 slice-done
  70.1 0.0 copy-done
  70.2 3.7 %convolution_convert_fusion.2 = bf16[512,1536]{1,0:T(8,128)(2,1)} fusion(bf16[512,1536]{1,0:T(8,128)(2,1)S(1)} %bitcast.16, bf16[1536,1536]{1,0:T(8,128)(2,1)S(1)} %bitcast.26), kind=kOutput, calls=%fused_computation.4 | convolution fusion | flops 2416705536 | bytes 7864320 | tf_op jit(solution)/shard_map/dot_general | solution.py:20
  73.9 36.1 %exchange1.1 = (bf16[4,128,1536]{2,1,0:T(8,128)(2,1)}, bf16[4,128,1536]{2,1,0:T(8,128)(2,1)}) custom-call(bf16[4,128,1536]{2,1,0:T(8,128)(2,1)} %bitcast.28, bf16[4,128,1536]{2,1,0:T(8,128)(2,1)} %bitcast.27), custom_call_target="tpu_custom_call" | custom-call | tf_op jit(solution)/shard_map/exchange1/pallas_call | solution.py:86
  110.0 2.6 convert_reduce_fusion
  112.6 1.2 fusion.5
  113.8 36.6 %exchange2.1 = (bf16[4,128,1536]{2,1,0:T(8,128)(2,1)}, bf16[4,128,1536]{2,1,0:T(8,128)(2,1)}) custom-call(bf16[128,1536]{1,0:T(8,128)(2,1)} %get-tuple-element.64.refs_0_, bf16[128,1536]{1,0:T(8,128)(2,1)} %get-tuple-element.63.refs_1_), custom_call_target="tpu_custom_call" | custom-call | tf_op jit(solution)/shard_map/exchange2/pallas_call | solution.py:86
  150.4 6.6 %squares.3 = f32[8,128]{1,0:T(8,128)} custom-call(bf16[512,1536]{1,0:T(8,128)(2,1)} %bitcast.23, bf16[512,1536]{1,0:T(8,128)(2,1)} %bitcast.18), custom_call_target="tpu_custom_call" | custom-call | tf_op jit(solution)/shard_map/squares/pallas_call | solution.py:127
  157.0 6.5 %squares.2 = f32[8,128]{1,0:T(8,128)} custom-call(bf16[512,1536]{1,0:T(8,128)(2,1)} %bitcast.14, bf16[512,1536]{1,0:T(8,128)(2,1)} %bitcast.20), custom_call_target="tpu_custom_call" | custom-call | tf_op jit(solution)/shard_map/squares/pallas_call | solution.py:127
  163.5 1.3 add.15.refs_1_
  164.8 6.1 %convolution_convert_fusion = bf16[512,1536]{1,0:T(8,128)(2,1)} fusion(bf16[512,1536]{1,0:T(8,128)(2,1)S(1)} %bitcast.22, bf16[1536,1536]{1,0:T(8,128)(2,1)} %weight_ref.2), kind=kOutput, calls=%fused_computation.2 | convolution fusion | flops 2416705536 | bytes 7864320 | tf_op jit(solution)/shard_map/dot_general | solution.py:20
  170.8 52.6 %exchange3.1 = (bf16[8,64,1536]{2,1,0:T(8,128)(2,1)}, f32[8,8,128]{2,1,0:T(8,128)}) custom-call(bf16[8,64,1536]{2,1,0:T(8,128)(2,1)} %bitcast.29, f32[8,128]{1,0:T(8,128)} %add.15.refs_1_), custom_call_target="tpu_custom_call" | custom-call | tf_op jit(solution)/shard_map/exchange3/pallas_call | solution.py:86
  223.5 2.4 reduce_sum.50
  225.8 1.4 reduce_sum.51.refs_0_
  227.2 4.0 %exchange4.1 = f32[4,8,128]{2,1,0:T(8,128)} custom-call(f32[8,128]{1,0:T(8,128)} %reduce_sum.51.refs_0_), custom_call_target="tpu_custom_call" | custom-call | tf_op jit(solution)/shard_map/exchange4/pallas_call | solution.py:86
  231.2 1.3 reduce_sum.52
  233.3 16.8 %moments.3 = (bf16[1536,1536]{1,0:T(8,128)(2,1)}, bf16[1536,1536]{1,0:T(8,128)(2,1)}, bf16[1536,1536]{1,0:T(8,128)(2,1)}, f32[2,1536]{1,0:T(2,128)}, f32[2,1536]{1,0:T(2,128)}) custom-call(f32[1,1]{1,0:T(1,128)} %bitcast.7.factor_ref, bf16[512,1536]{1,0:T(8,128)(2,1)} %bitcast.24, bf16[512,1536]{1,0:T(8,128)(2,1)} %bitcast.19, ...), custom_call_target="tpu_custom_call" | custom-call | tf_op jit(solution)/shard_map/moments/pallas_call | solution.py:184
  250.0 16.7 %moments.2 = (bf16[1536,1536]{1,0:T(8,128)(2,1)}, bf16[1536,1536]{1,0:T(8,128)(2,1)}, bf16[1536,1536]{1,0:T(8,128)(2,1)}, f32[2,1536]{1,0:T(2,128)}, f32[2,1536]{1,0:T(2,128)}) custom-call(f32[1,1]{1,0:T(1,128)} %bitcast.7.factor_ref, bf16[512,1536]{1,0:T(8,128)(2,1)} %bitcast.15, bf16[512,1536]{1,0:T(8,128)(2,1)} %bitcast.21, ...), custom_call_target="tpu_custom_call" | custom-call | tf_op jit(solution)/shard_map/moments/pallas_call | solution.py:184
  266.7 8.8 %exchange5.1 = (f32[8,2,1536]{2,1,0:T(2,128)}, f32[8,2,1536]{2,1,0:T(2,128)}, f32[4,2,1536]{2,1,0:T(2,128)}, f32[4,2,1536]{2,1,0:T(2,128)}) custom-call(f32[2,1536]{1,0:T(2,128)} %get-tuple-element.48.refs_0_, f32[2,1536]{1,0:T(2,128)} %get-tuple-element.49.refs_1_, f32[2,1536]{1,0:T(2,128)} %get-tuple-element.50.refs_2_, f32[2,1536]{1,0:T(2,128)} %get-tuple-element.51.refs_3_), custom_call_target="tpu_custom_call" | custom-call | tf_op jit(solution)/shard_map/exchange5/pallas_call | solution.py:86
  275.5 0.9 reduce_max.36
  276.5 0.6 broadcast_maximum_fusion.3.row_ref
  277.1 0.8 reduce_max.37
  277.9 0.6 broadcast_maximum_fusion.2.col_ref
  278.5 9.3 %encode.2 = (bf16[1536,1536]{1,0:T(8,128)(2,1)}, bf16[1536,1536]{1,0:T(8,128)(2,1)}) custom-call(bf16[1536,1536]{1,0:T(8,128)(2,1)} %get-tuple-element.46.moment_ref, bf16[1536,1536]{1,0:T(8,128)(2,1)} %get-tuple-element.47.second_ref, f32[2,1536]{1,0:T(2,128)} %broadcast_maximum_fusion.3.row_ref, f32[2,1536]{1,0:T(2,128)} %broadcast_maximum_fusion.2.col_ref), custom_call_target="tpu_custom_call" | custom-call | tf_op jit(solution)/shard_map/encode/pallas_call | solution.py:235
  287.9 0.6 broadcast_maximum_fusion.col_ref
  288.5 0.6 broadcast_maximum_fusion.1.row_ref
  289.1 9.2 %encode.3 = (bf16[1536,1536]{1,0:T(8,128)(2,1)}, bf16[1536,1536]{1,0:T(8,128)(2,1)}) custom-call(bf16[1536,1536]{1,0:T(8,128)(2,1)} %get-tuple-element.57.moment_ref, bf16[1536,1536]{1,0:T(8,128)(2,1)} %get-tuple-element.58.second_ref, f32[2,1536]{1,0:T(2,128)} %broadcast_maximum_fusion.1.row_ref, f32[2,1536]{1,0:T(2,128)} %broadcast_maximum_fusion.col_ref), custom_call_target="tpu_custom_call" | custom-call | tf_op jit(solution)/shard_map/encode/pallas_call | solution.py:235
  (12 shorter events, 0.1 us)
Async XLA Ops:
  0.6 69.5 %slice-start = ((s8[4718592]{0:T(1024)(128)(4,1)}), s8[524288]{0:T(1024)(128)(4,1)S(1)}, s32[]{:S(2)}) async-start(s8[4718592]{0:T(1024)(128)(4,1)} %bitcast.25), calls=%async_computation | async-start | bytes 1048576
  63.4 6.8 %copy-start = (bf16[8,64,1536]{2,1,0:T(8,128)(2,1)S(1)}, bf16[8,64,1536]{2,1,0:T(8,128)(2,1)}, u32[]{:S(2)}) copy-start(bf16[8,64,1536]{2,1,0:T(8,128)(2,1)} %get-tuple-element.37) | copy-start | bytes 4718596
  63.4 6.8 %slice-start.1 = ((s8[4718592]{0:T(1024)(128)(4,1)}), s8[4194304]{0:T(1024)(128)(4,1)S(1)}, s32[]{:S(2)}) async-start(s8[4718592]{0:T(1024)(128)(4,1)} %bitcast.25), calls=%async_computation.1 | async-start | bytes 8388608
  150.4 14.4 %copy-start.1 = (bf16[4,128,1536]{2,1,0:T(8,128)(2,1)S(1)}, bf16[4,128,1536]{2,1,0:T(8,128)(2,1)}, u32[]{:S(2)}) copy-start(bf16[4,128,1536]{2,1,0:T(8,128)(2,1)} %get-tuple-element.41) | copy-start | bytes 4718596
  157.0 6.5 %copy-start.4 = (f32[8,128]{1,0:T(8,128)S(1)}, f32[8,128]{1,0:T(8,128)}, u32[]{:S(2)}) copy-start(f32[8,128]{1,0:T(8,128)} %squares.3) | copy-start | bytes 12292
  278.5 9.3 %copy-start.3 = (f32[4,2,1536]{2,1,0:T(2,128)S(1)}, f32[4,2,1536]{2,1,0:T(2,128)}, u32[]{:S(2)}) copy-start(f32[4,2,1536]{2,1,0:T(2,128)} %get-tuple-element.59) | copy-start | bytes 147460
  278.5 9.3 %copy-start.2 = (f32[8,2,1536]{2,1,0:T(2,128)S(1)}, f32[8,2,1536]{2,1,0:T(2,128)}, u32[]{:S(2)}) copy-start(f32[8,2,1536]{2,1,0:T(2,128)} %get-tuple-element.60) | copy-start | bytes 294916
where the time goes:
time: 299 us; the launch traced here: 298 us
  Pallas kernels  266 us (89%)
  matrix products  16.5 us (6%)
  other arithmetic  14.4 us (5%)
    pallas_call x6, Pallas kernels, exchange(): pl.pallas_call(functools.partial(exchange_kernel, plan, sizes), out_shape...  201 us
    pallas_call x2, Pallas kernels, moments(): pl.pallas_call(moments_kernel, grid=(rows // block,), out_shape=[half, ha...  33.4 us
    pallas_call x2, Pallas kernels, encode(): pl.pallas_call(encode_kernel, grid=(rows // block,), out_shape=[half, hal...  18.5 us
    dot_general x3, matrix products, contract(): lax.dot_general(left, right, (((left_dim,), (right_dim,)), ((), ())), pre...  16.5 us
    pallas_call x2, Pallas kernels, squares(): pl.pallas_call(squares_kernel, grid=(rows // block,), out_shape=jax.Shape...  13.1 us

commit v1 on v0

--- a/solution.py
+++ b/solution.py
@@ -28,6 +28,497 @@
     hidden = (preact * cumulative).astype(jnp.bfloat16)
     delta = (hidden_grad * (cumulative + preact * density)).astype(jnp.bfloat16)
     return (hidden, delta)
+
+
+MESH = pl.DeviceIdType.MESH
+
+
+def remote(source, target, send, receive, axis, peer):
+    return pltpu.make_async_remote_copy(
+        src_ref=source,
+        dst_ref=target,
+        send_sem=send,
+        recv_sem=receive,
+        device_id={axis: peer},
+        device_id_type=MESH,
+    )
+
+
+def span(start, size):
+    return pl.ds(pl.multiple_of(start, size), size)
+
+
+def lane_tile(size):
+    return 512 if size % 512 == 0 else 256 if size % 256 == 0 else 128
+
+
+def folded(values):
+    total = values[:8, :LANES] * 0.0
+    for low in range(0, values.shape[0], 8):
+        for at in range(0, values.shape[1], LANES):
+            total = total + values[low : low + 8, at : at + LANES]
+    return total
+
+
+def front_kernel(
+    shape, x_ref, c_ref, wi_hbm, wo_hbm,
+    x_out, c_out, hidden_out, delta_out, grad_ref, factor_ref,
+    acts, wi, wo, pair_send, pair_recv, pair_own, line_send, line_recv, line_own, hd,
+    dx_own, dx_send, dx_recv, dz_send, dz_recv, part_ref, col_tops, row_tops, grams,
+    load_sem, z_send, z_recv, y_send, y_recv, pair_s, pair_r, line_s, line_r,
+    gather_s, gather_r, share_s, share_r, dy_s, dy_r, dz_s, dz_r,
+    tot_s, tot_r, row_s, row_r, out_sem,
+):
+    rows, cols, nx, ny, nz, entries = shape
+    t, width = x_ref.shape
+    hidden = wi.shape[1]
+    size = ny * t
+    half = size // 2
+    piece = half // nx
+    tokens = size * nz
+    r, k = lax.axis_index("row"), lax.axis_index("col")
+    x, core = r // 2, r % 2
+    z, y = k // ny, k % ny
+    partner = x * 2 + (1 - core)
+    below, above = z, nz - 1 - z
+    middle = jnp.minimum(below, above)
+
+    def source_of(g):
+        if g == 0:
+            return z, 0
+        near = g <= 2 * middle
+        distance = jnp.where(near, (g + 1) // 2, g - middle)
+        side = jnp.where(near, -1 if g % 2 else 1, jnp.where(above > below, 1, -1))
+        return z + side * distance, side
+
+    order = [source_of(g) for g in range(nz)]
+
+    def line_peer(off):
+        return lax.rem(x + off, nx) * 2 + core
+
+    def y_peer(off):
+        return z * ny + lax.rem(y + off, ny)
+
+    loads = [
+        pltpu.make_async_copy(x_ref, acts.at[0, span(k * t, t)], load_sem.at[0]),
+        pltpu.make_async_copy(c_ref, acts.at[1, span(k * t, t)], load_sem.at[1]),
+        pltpu.make_async_copy(wi_hbm, wi, load_sem.at[2]),
+        pltpu.make_async_copy(wo_hbm, wo, load_sem.at[3]),
+    ]
+    for load in loads:
+        load.start()
+    barrier = pltpu.get_barrier_semaphore()
+    for off in range(1, cols):
+        pl.semaphore_signal(
+            barrier, inc=1, device_id={"col": lax.rem(k + off, cols)}, device_id_type=MESH
+        )
+    for off in range(1, rows):
+        pl.semaphore_signal(
+            barrier, inc=1, device_id={"row": lax.rem(r + off, rows)}, device_id_type=MESH
+        )
+    loads[0].wait()
+    loads[1].wait()
+    pl.semaphore_wait(barrier, cols + rows - 2)
+
+    pending = []
+
+    def z_copy(item, zs, g, way, sign):
+        block = acts.at[item, span((zs * ny + y) * t, t)]
+        return remote(
+            block, block, z_send.at[item, g, way], z_recv.at[item, zs], "col", (z + sign) * ny + y
+        )
+
+    def y_copies(item, zs, g):
+        block = acts.at[item, span((zs * ny + y) * t, t)]
+        copies = [
+            remote(
+                block, block, y_send.at[item, g, off], y_recv.at[item, zs, y], "col", y_peer(off)
+            )
+            for off in range(1, ny)
+        ]
+        for copy in copies:
+            copy.start()
+            pending.append(copy)
+
+    ways = ((0, 1, z < nz - 1), (1, -1, z > 0))
+    for item in range(2):
+        for way, sign, there in ways:
+            pl.when(there)(lambda i=item, w=way, s=sign: z_copy(i, z, 0, w, s).start())
+        y_copies(item, z, 0)
+
+    def onward(g):
+        zs, side = order[g]
+        ahead = z - side
+        return zs, -side, jnp.logical_and(ahead >= 0, ahead < nz)
+
+    def forward(g):
+        zs, sign, there = onward(g)
+        for item in range(2):
+            block = acts.at[item, span((zs * ny + y) * t, t)]
+            remote(
+                block, block, z_send.at[item, g, 0], z_recv.at[item, zs], "col", y_peer(1)
+            ).wait_recv()
+            pl.when(there)(lambda i=item: z_copy(i, zs, g, 0, sign).start())
+            y_copies(item, zs, g)
+
+    def y_wait(g, item):
+        zs, _ = order[g]
+        for off in range(1, ny):
+            ys = lax.rem(y + off, ny)
+            block = acts.at[item, span((zs * ny + ys) * t, t)]
+            remote(
+                block, block, y_send.at[item, g, off], y_recv.at[item, zs, ys], "col", y_peer(1)
+            ).wait_recv()
+
+    tile_h, tile_w = lane_tile(hidden), lane_tile(width)
+
+    def forward_product(g, item):
+        first = order[g][0] * size
+        left = jnp.concatenate(
+            [
+                acts[item, span(first + (1 - core) * half, half), :],
+                acts[item, span(first + core * half, half), :],
+            ],
+            axis=0,
+        )
+
+        @pl.loop(0, hidden // tile_h)
+        def _(n):
+            at = span(n * tile_h, tile_h)
+            if item == 0:
+                part = contract(left, wi[:, at], 1, 0)
+            else:
+                part = contract(left, wo[at, :], 1, 1)
+            pair_send[g, item, :, at] = part[:half]
+            pair_own[g, item, :, at] = part[half:]
+
+        pair_copy(g, item).start()
+        pending.append(pair_copy(g, item))
+
+    def pair_copy(g, item):
+        return remote(
+            pair_send.at[g, item], pair_recv.at[g, item],
+            pair_s.at[g, item], pair_r.at[g, item], "row", partner,
+        )
+
+    def line_copy(g, off):
+        return remote(
+            line_send.at[g, off - 1], line_recv.at[g, off - 1],
+            line_s.at[g, off], line_r.at[g, off], "row", line_peer(off),
+        )
+
+    def pair_sum(g):
+        for item in range(2):
+            pair_copy(g, item).wait_recv()
+        for off in range(1, nx):
+            take = span(lax.rem(x + off, nx) * piece, piece)
+            for item in range(2):
+                line_send[g, off - 1, item] = (
+                    pair_own[g, item, take, :] + pair_recv[g, item, take, :]
+                ).astype(jnp.bfloat16)
+            line_copy(g, off).start()
+            pending.append(line_copy(g, off))
+        take = span(x * piece, piece)
+        for item in range(2):
+            line_own[g, item] = pair_own[g, item, take, :] + pair_recv[g, item, take, :]
+
+    def gather_block(g, xs):
+        return hd.at[:, span(order[g][0] * size + core * half + xs * piece, piece), :]
+
+    def gather_copy(g, off):
+        block = gather_block(g, x)
+        return remote(
+            block, block, gather_s.at[g, off], gather_r.at[g, off], "row", line_peer(off)
+        )
+
+    def active(g):
+        for off in range(1, nx):
+            line_copy(g, off).wait_recv()
+        first = order[g][0] * size + core * half + x * piece
+
+        @pl.loop(0, hidden // LANES)
+        def _(n):
+            at = span(n * LANES, LANES)
+            preact, hidden_grad = line_own[g, 0, :, at], line_own[g, 1, :, at]
+            for off in range(1, nx):
+                preact = preact + line_recv[g, off - 1, 0, :, at].astype(jnp.float32)
+                hidden_grad = hidden_grad + line_recv[g, off - 1, 1, :, at].astype(jnp.float32)
+            value, slope = activate(preact, hidden_grad)
+            hd[0, span(first, piece), at] = value
+            hd[1, span(first, piece), at] = slope
+
+        for off in range(1, nx):
+            gather_copy(g, off).start()
+            pending.append(gather_copy(g, off))
+
+    def share_copy(g, which):
+        block = hd.at[:, span(order[g][0] * size + which * half, half), :]
+        return remote(block, block, share_s.at[g], share_r.at[g], "row", partner)
+
+    def share(g):
+        for off in range(1, nx):
+            xs = lax.rem(x + nx - off, nx)
+            block = gather_block(g, xs)
+            remote(
+                block, block, gather_s.at[g, off], gather_r.at[g, off], "row", line_peer(off)
+            ).wait_recv()
+        share_copy(g, core).start()
+        pending.append(share_copy(g, core))
+
+    def share_wait(g):
+        share_copy(g, 1 - core).wait_recv()
+
+    def dx_copy(g, off):
+        return remote(
+            dx_send.at[g, off - 1], dx_recv.at[g, off - 1],
+            dy_s.at[g, off], dy_r.at[g, off], "col", y_peer(off),
+        )
+
+    def back_product(groups):
+        left = jnp.concatenate(
+            [
+                hd[1, span(order[g][0] * size + lax.rem(y + off, ny) * t, t), :]
+                for g in groups
+                for off in range(ny)
+            ],
+            axis=0,
+        )
+
+        @pl.loop(0, width // tile_w)
+        def _(n):
+            at = span(n * tile_w, tile_w)
+            part = contract(left, wi[at, :], 1, 1)
+            for i, g in enumerate(groups):
+                for off in range(ny):
+                    low = (i * ny + off) * t
+                    if off == 0:
+                        dx_own[g, :, at] = part[low : low + t]
+                    else:
+                        dx_send[g, off - 1, :, at] = part[low : low + t].astype(jnp.bfloat16)
+
+        for g in groups:
+            for off in range(1, ny):
+                dx_copy(g, off).start()
+                pending.append(dx_copy(g, off))
+
+    def dz_copy(g):
+        return remote(
+            dz_send.at[g], dz_recv.at[z], dz_s.at[g], dz_r.at[z], "col", order[g][0] * ny + y
+        )
+
+    def back_sum(g):
+        for off in range(1, ny):
+            dx_copy(g, off).wait_recv()
+        total = dx_own[g]
+        for off in range(1, ny):
+            total = total + dx_recv[g, off - 1].astype(jnp.float32)
+        if g == 0:
+            dx_own[0] = total
+        else:
+            dz_send[g] = total.astype(jnp.bfloat16)
+            dz_copy(g).start()
+            pending.append(dz_copy(g))
+
+    outs = []
+
+    def put(source, target, slot):
+        copy = pltpu.make_async_copy(source, target, out_sem.at[slot])
+        copy.start()
+        outs.append(copy)
+
+    use_grams = grams is not None
+    tile_t = 256 if tokens % 256 == 0 else 128
+
+    def gram(which, source, item):
+        @pl.loop(0, tokens // tile_t)
+        def _(n):
+            at = span(n * tile_t, tile_t)
+            grams[which, :, at] = contract(source[item], source[item, at, :], 1, 1)
+
+    def local_total():
+        if use_grams:
+            part_ref[...] = jnp.zeros_like(part_ref)
+
+            @pl.loop(0, tokens // tile_t)
+            def _(n):
+                at = span(n * tile_t, tile_t)
+                late_in = contract(hd[1], hd[1, at, :], 1, 1)
+                part_ref[...] += folded(late_in * grams[0, :, at])
+                late_out = contract(hd[0], hd[0, at, :], 1, 1)
+                part_ref[...] += folded(late_out * grams[1, :, at])
+        else:
+            part_ref[...] = jnp.zeros_like(part_ref)
+            for left, right, count in ((acts.at[0], hd.at[1], width), (hd.at[0], acts.at[1], hidden)):
+
+                @pl.loop(0, count // LANES)
+                def _(n):
+                    at = span(n * LANES, LANES)
+                    part = contract(left[:, at], right[...], 0, 0)
+                    part_ref[...] += folded(part * part)
+
+    for s in range(nz + 3):
+        if s + 1 < nz:
+            forward(s + 1)
+        if s < nz:
+            for item in range(2):
+                y_wait(s, item)
+                if s == 0:
+                    loads[2 + item].wait()
+                forward_product(s, item)
+        if 0 <= s - 1 < nz:
+            active(s - 1)
+        if s == nz - 1:
+            put(acts.at[0], x_out, 0)
+            put(acts.at[1], c_out, 1)
+        if s < nz:
+            pair_sum(s)
+        if s == nz and use_grams:
+            gram(0, acts, 0)
+            gram(1, acts, 1)
+        if 0 <= s - 2 < nz:
+            share(s - 2)
+        if 0 <= s - 3 < nz:
+            share_wait(s - 3)
+        if s == nz - 1:
+            back_product(list(range(nz - 3)))
+        if s == nz:
+            back_product([nz - 3])
+            for g in range(nz - 3):
+                back_sum(g)
+        if s == nz + 1:
+            back_product([nz - 2])
+            back_sum(nz - 3)
+    put(hd.at[0], hidden_out, 2)
+    put(hd.at[1], delta_out, 3)
+    back_product([nz - 1])
+    local_total()
+
+    def col_copy(off):
+        return remote(
+            part_ref, col_tops.at[off], tot_s.at[off], tot_r.at[off],
+            "col", lax.rem(k + off, cols),
+        )
+
+    def row_copy(off):
+        return remote(
+            col_tops.at[0], row_tops.at[off], row_s.at[off], row_r.at[off],
+            "row", lax.rem(r + off, rows),
+        )
+
+    for off in range(1, cols):
+        col_copy(off).start()
+        pending.append(col_copy(off))
+    back_sum(nz - 2)
+    back_sum(nz - 1)
+    for off in range(1, cols):
+        col_copy(off).wait_recv()
+    total = part_ref[...]
+    for off in range(1, cols):
+        total = total + col_tops[off]
+    col_tops[0] = total
+    for off in range(1, rows):
+        row_copy(off).start()
+        pending.append(row_copy(off))
+    for off in range(1, rows):
+        row_copy(off).wait_recv()
+        total = total + row_tops[off]
+    total = jnp.sum(jnp.sum(total, axis=0, keepdims=True), axis=1, keepdims=True)
+    total = jnp.maximum(total, 0.0)
+    factor = 1.0 / jnp.maximum(jnp.sqrt(total / entries), 1.0)
+    factor_ref[...] = jnp.broadcast_to(factor, factor_ref.shape)
+
+    total = dx_own[0]
+    for off in range(1, nz):
+        zs = lax.rem(z + off, nz)
+        remote(
+            dz_send.at[1], dz_recv.at[zs], dz_s.at[1], dz_r.at[zs], "col", y_peer(1)
+        ).wait_recv()
+        total = total + dz_recv[zs].astype(jnp.float32)
+    grad_ref[...] = total.astype(jnp.bfloat16)
+
+    for item in range(2):
+        for way, sign, there in ways:
+            pl.when(there)(lambda i=item, w=way, s=sign: z_copy(i, z, 0, w, s).wait_send())
+    for g in range(1, nz):
+        zs, sign, there = onward(g)
+        for item in range(2):
+            pl.when(there)(lambda i=item, a=zs, b=g, s=sign: z_copy(i, a, b, 0, s).wait_send())
+    for copy in pending:
+        copy.wait_send()
+    for copy in outs:
+        copy.wait()
+
+
+def front(sizes, inputs, cotangent, weight_in, weight_out):
+    rows, cols = sizes["row"], sizes["col"]
+    nx = rows // 2
+    ny = 2 ** ((cols.bit_length() - 1) // 2)
+    nz = cols // ny
+    t, width = inputs.shape
+    hidden = weight_in.shape[1]
+    size = t * ny
+    half, tokens = size // 2, size * nz
+    piece = half // nx
+    entries = 2.0 * width * rows * hidden * cols
+    bf, f4 = jnp.bfloat16, jnp.float32
+    use_grams = tokens <= hidden
+    dma = lambda *dims: pltpu.SemaphoreType.DMA(dims)
+    scratch = [
+        pltpu.VMEM((2, tokens, width), bf),
+        pltpu.VMEM(weight_in.shape, bf),
+        pltpu.VMEM(weight_out.shape, bf),
+        pltpu.VMEM((nz, 2, half, hidden), f4),
+        pltpu.VMEM((nz, 2, half, hidden), f4),
+        pltpu.VMEM((nz, 2, half, hidden), f4),
+        pltpu.VMEM((nz, nx - 1, 2, piece, hidden), bf),
+        pltpu.VMEM((nz, nx - 1, 2, piece, hidden), bf),
+        pltpu.VMEM((nz, 2, piece, hidden), f4),
+        pltpu.VMEM((2, tokens, hidden), bf),
+        pltpu.VMEM((nz, t, width), f4),
+        pltpu.VMEM((nz, ny - 1, t, width), bf),
+        pltpu.VMEM((nz, ny - 1, t, width), bf),
+        pltpu.VMEM((nz, t, width), bf),
+        pltpu.VMEM((nz, t, width), bf),
+        pltpu.VMEM((8, LANES), f4),
+        pltpu.VMEM((cols, 8, LANES), f4),
+        pltpu.VMEM((rows, 8, LANES), f4),
+        pltpu.VMEM((2, tokens, tokens), f4) if use_grams else None,
+        dma(4),
+        dma(2, nz, 2), dma(2, nz), dma(2, nz, ny), dma(2, nz, ny),
+        dma(nz, 2), dma(nz, 2), dma(nz, nx), dma(nz, nx),
+        dma(nz, nx), dma(nz, nx), dma(nz), dma(nz),
+        dma(nz, ny), dma(nz, ny), dma(nz), dma(nz),
+        dma(cols), dma(cols), dma(rows), dma(rows), dma(4),
+    ]
+    kept = [item for item in scratch if item is not None]
+    slot = 10 + scratch.index(None) if None in scratch else None
+
+    def kernel(*refs):
+        refs = list(refs)
+        if slot is not None:
+            refs.insert(slot, None)
+        front_kernel((rows, cols, nx, ny, nz, entries), *refs)
+
+    anywhere = pl.BlockSpec(memory_space=pl.ANY)
+    inside = pl.BlockSpec(memory_space=pltpu.VMEM)
+    return pl.pallas_call(
+        kernel,
+        out_shape=[
+            jax.ShapeDtypeStruct((tokens, width), bf),
+            jax.ShapeDtypeStruct((tokens, width), bf),
+            jax.ShapeDtypeStruct((tokens, hidden), bf),
+            jax.ShapeDtypeStruct((tokens, hidden), bf),
+            jax.ShapeDtypeStruct((t, width), bf),
+            jax.ShapeDtypeStruct((8, LANES), f4),
+        ],
+        in_specs=[anywhere] * 4,
+        out_specs=[anywhere] * 4 + [inside] * 2,
+        scratch_shapes=kept,
+        compiler_params=pltpu.CompilerParams(
+            collective_id=0, has_side_effects=True, vmem_limit_bytes=60 * 2**20
+        ),
+        name="front",
+    )(inputs, cotangent, weight_in, weight_out)
 
 
 def exchange_kernel(plan, sizes, *refs):
@@ -105,36 +596,8 @@
     return folded
 
 
-def squares_kernel(left_ref, right_ref, total_ref):
-    gradient = contract(left_ref[...], right_ref[...], 0, 0)
-    folded = lane_fold(gradient * gradient, jnp.add)
-    folded = jnp.sum(folded.reshape(-1, 8, LANES), axis=0)
-
-    @pl.when(pl.program_id(0) == 0)
-    def _():
-        total_ref[...] = jnp.zeros_like(total_ref)
-
-    total_ref[...] += folded
-
-
 def row_block(rows):
     return 256 if rows % 256 == 0 else 128
-
-
-def squares(left, right):
-    tokens, rows = left.shape
-    block = row_block(rows)
-    return pl.pallas_call(
-        squares_kernel,
-        grid=(rows // block,),
-        out_shape=jax.ShapeDtypeStruct((8, LANES), jnp.float32),
-        in_specs=[
-            pl.BlockSpec((tokens, block), lambda i: (0, i)),
-            pl.BlockSpec(right.shape, lambda i: (0, 0)),
-        ],
-        out_specs=pl.BlockSpec((8, LANES), lambda i: (0, 0)),
-        name="squares",
-    )(left, right)
 
 
 def to_lanes(column_tops):
@@ -150,7 +613,7 @@
     update_ref, new_moment_ref, new_second_ref, row_ref, col_ref,
 ):
     gradient = contract(left_ref[...], right_ref[...], 0, 0)
-    scaled = gradient * factor_ref[0, 0]
+    scaled = gradient * factor_ref[0:1, 0:1]
     moment_new = momentum_decay * moment_ref[...].astype(jnp.float32) + (
         1.0 - momentum_decay
     ) * scaled
@@ -192,7 +655,7 @@
             jax.ShapeDtypeStruct((2, cols), jnp.float32),
         ],
         in_specs=[
-            pl.BlockSpec(memory_space=pltpu.SMEM),
+            pl.BlockSpec((8, LANES), lambda i: (0, 0)),
             pl.BlockSpec((tokens, block), lambda i: (0, i)),
             pl.BlockSpec((tokens, cols), lambda i: (0, 0)),
             tile,
@@ -250,46 +713,9 @@
 def shards(
     sizes, inputs, cotangent, weight_in, moment_in, second_in, weight_out, moment_out, second_out
 ):
-    rows, cols = sizes["row"], sizes["col"]
-    width_in, hidden_cols = weight_in.shape
-    width = inputs.shape[1]
-    tokens = inputs.shape[0] * cols
-    entries = 2.0 * width_in * rows * hidden_cols * cols
-    all_inputs, all_cotangent = exchange(
-        0, (("col", False), ("col", False)), sizes, inputs, cotangent
-    )
-    all_inputs = all_inputs.reshape(tokens, width)
-    all_cotangent = all_cotangent.reshape(tokens, width)
-    preact_part = contract(all_inputs, weight_in, 1, 0).astype(jnp.bfloat16)
-    grad_part = contract(all_cotangent, weight_out, 1, 1).astype(jnp.bfloat16)
-    parts = (rows, tokens // rows, hidden_cols)
-    preact_parts, grad_parts = exchange(
-        1,
-        (("row", True), ("row", True)),
-        sizes,
-        preact_part.reshape(parts),
-        grad_part.reshape(parts),
-    )
-    preact = jnp.sum(preact_parts.astype(jnp.float32), axis=0)
-    hidden_grad = jnp.sum(grad_parts.astype(jnp.float32), axis=0)
-    hidden, delta = activate(preact, hidden_grad)
-    all_hidden, all_delta = exchange(2, (("row", False), ("row", False)), sizes, hidden, delta)
-    all_hidden = all_hidden.reshape(tokens, hidden_cols)
-    all_delta = all_delta.reshape(tokens, hidden_cols)
-    grad_input_part = contract(all_delta, weight_in, 1, 1).astype(jnp.bfloat16)
-    local_total = squares(all_inputs, all_delta) + squares(all_hidden, all_cotangent)
-    grad_input_parts, totals = exchange(
-        3,
-        (("col", True), ("col", False)),
-        sizes,
-        grad_input_part.reshape(cols, tokens // cols, width),
-        local_total,
-    )
-    input_grad = jnp.sum(grad_input_parts.astype(jnp.float32), axis=0).astype(jnp.bfloat16)
-    (totals,) = exchange(4, (("row", False),), sizes, jnp.sum(totals, axis=0))
-    total = jnp.sum(totals)
-    factor = 1.0 / jnp.maximum(jnp.sqrt(total / entries), 1.0)
-    factor = factor.reshape(1, 1)
+    all_inputs, all_cotangent, all_hidden, all_delta, input_grad, factor = front(
+        sizes, inputs, cotangent, weight_in, weight_out
+    )
     update_in, moment_new_in, second_new_in, rows_in, cols_in = moments(
         factor, all_inputs, all_delta, weight_in, moment_in, second_in
     )

time: 299 us -> 158 us (0.53)
  Pallas kernels: 266 us -> 153 us
  matrix products: 16.5 us -> 0 us
  other arithmetic: 14.4 us -> 3.06 us
    pallas_call x6 -> x1, Pallas kernels: 201 us -> 9.72 us  [exchange(): pl.pallas_call(functools.partial(exchange_kernel, plan, sizes), out_shape...]
    pallas_call x2 -> x1, Pallas kernels: 13.1 us -> 91.3 us  [front(): pl.pallas_call(kernel, out_shape=[jax.ShapeDtypeStruct((tokens, width), b...]
    dot_general x3 -> x0, matrix products: 16.5 us -> none  [contract(): lax.dot_general(left, right, (((left_dim,), (right_dim,)), ((), ())), pre...]
    reduce_sum x4 -> x0, other arithmetic: 7.62 us -> none  [the longest x1 2.58 us: shards(): hidden_grad = jnp.sum(grad_parts.astype(jnp.float32), axis=0)]
where the time goes in v1:
time: 158 us; the launch traced here: 157 us
  Pallas kernels  153 us (97%)
  other arithmetic  3.06 us (2%)
    pallas_call x1, Pallas kernels, front(): pl.pallas_call(kernel, out_shape=[jax.ShapeDtypeStruct((tokens, width), b...  91.3 us
    pallas_call x2, Pallas kernels, moments(): pl.pallas_call(moments_kernel, grid=(rows // block,), out_shape=[half, ha...  33.4 us
    pallas_call x2, Pallas kernels, encode(): pl.pallas_call(encode_kernel, grid=(rows // block,), out_shape=[half, hal...  18.5 us
    pallas_call x1, Pallas kernels, exchange(): pl.pallas_call(functools.partial(exchange_kernel, plan, sizes), out_shape...  9.72 us

profile of v1, /device:TPU:0, one launch (start us, length us, event | category | flops | bytes accessed | tf_op | source)
XLA Modules:
  0.0 157.3 jit_solution(11583849086214281471)
XLA Ops:
  0.6 91.3 %front.1 = (bf16[512,1536]{1,0:T(8,128)(2,1)}, bf16[512,1536]{1,0:T(8,128)(2,1)}, bf16[512,1536]{1,0:T(8,128)(2,1)}, bf16[512,1536]{1,0:T(8,128)(2,1)}, bf16[64,1536]{1,0:T(8,128)(2,1)}, /*index=5*/f32[8,128]{1,0:T(8,128)}) custom-call(bf16[64,1536]{1,0:T(8,128)(2,1)} %refs_0_.1, bf16[64,1536]{1,0:T(8,128)(2,1)} %refs_1_.1, bf16[1536,1536]{1,0:T(8,128)(2,1)} %weight_ref.2, ...), custom_call_target="tpu_custom_call" | custom-call | tf_op jit(solution)/shard_map/front/pallas_call | solution.py:504
  91.9 16.7 %moments.2 = (bf16[1536,1536]{1,0:T(8,128)(2,1)}, bf16[1536,1536]{1,0:T(8,128)(2,1)}, bf16[1536,1536]{1,0:T(8,128)(2,1)}, f32[2,1536]{1,0:T(2,128)}, f32[2,1536]{1,0:T(2,128)}) custom-call(f32[8,128]{1,0:T(8,128)} %get-tuple-element.36.factor_ref, bf16[512,1536]{1,0:T(8,128)(2,1)} %get-tuple-element.37.left_ref, ...), custom_call_target="tpu_custom_call" | custom-call | tf_op jit(solution)/shard_map/moments/pallas_call | solution.py:647
  108.6 16.8 %moments.3 = (bf16[1536,1536]{1,0:T(8,128)(2,1)}, bf16[1536,1536]{1,0:T(8,128)(2,1)}, bf16[1536,1536]{1,0:T(8,128)(2,1)}, f32[2,1536]{1,0:T(2,128)}, f32[2,1536]{1,0:T(2,128)}) custom-call(f32[8,128]{1,0:T(8,128)} %get-tuple-element.36.factor_ref, bf16[512,1536]{1,0:T(8,128)(2,1)} %get-tuple-element.43.left_ref, ...), custom_call_target="tpu_custom_call" | custom-call | tf_op jit(solution)/shard_map/moments/pallas_call | solution.py:647
  125.3 9.7 %exchange5.1 = (f32[8,2,1536]{2,1,0:T(2,128)}, f32[8,2,1536]{2,1,0:T(2,128)}, f32[4,2,1536]{2,1,0:T(2,128)}, f32[4,2,1536]{2,1,0:T(2,128)}) custom-call(f32[2,1536]{1,0:T(2,128)} %get-tuple-element.42.refs_0_, f32[2,1536]{1,0:T(2,128)} %get-tuple-element.45.refs_1_, f32[2,1536]{1,0:T(2,128)} %get-tuple-element.46.refs_2_, f32[2,1536]{1,0:T(2,128)} %get-tuple-element.47.refs_3_), custom_call_target="tpu_custom_call" | custom-call | tf_op jit(solution)/shard_map/exchange5/pallas_call | solution.py:577
  135.1 0.9 reduce_max.36
  136.0 0.8 reduce_max.37
  136.8 0.6 broadcast_maximum_fusion.2
  137.4 0.0 copy-start.2
  137.4 0.0 copy-start.1
  137.4 9.3 %encode.2 = (bf16[1536,1536]{1,0:T(8,128)(2,1)}, bf16[1536,1536]{1,0:T(8,128)(2,1)}) custom-call(bf16[1536,1536]{1,0:T(8,128)(2,1)} %get-tuple-element.40.moment_ref, bf16[1536,1536]{1,0:T(8,128)(2,1)} %get-tuple-element.41.second_ref, f32[2,1536]{1,0:T(2,128)} %get-tuple-element.78.row_ref, f32[2,1536]{1,0:T(2,128)} %get-tuple-element.79.col_ref), custom_call_target="tpu_custom_call" | custom-call | tf_op jit(solution)/shard_map/encode/pallas_call | solution.py:698
  146.7 0.0 copy-done.2
  146.7 0.0 copy-done.1
  146.8 0.6 broadcast_maximum_fusion
  147.4 0.0 copy-start
  147.4 9.2 %encode.3 = (bf16[1536,1536]{1,0:T(8,128)(2,1)}, bf16[1536,1536]{1,0:T(8,128)(2,1)}) custom-call(bf16[1536,1536]{1,0:T(8,128)(2,1)} %get-tuple-element.53.moment_ref, bf16[1536,1536]{1,0:T(8,128)(2,1)} %get-tuple-element.54.second_ref, f32[2,1536]{1,0:T(2,128)} %get-tuple-element.83.row_ref, f32[2,1536]{1,0:T(2,128)} %get-tuple-element.84.col_ref), custom_call_target="tpu_custom_call" | custom-call | tf_op jit(solution)/shard_map/encode/pallas_call | solution.py:698
  156.7 0.0 copy-done
  156.7 0.7 copy.20
  (2 shorter events, 0.1 us)
Async XLA Ops:
  137.4 9.3 %copy-start.2 = (f32[4,2,1536]{2,1,0:T(2,128)S(1)}, f32[4,2,1536]{2,1,0:T(2,128)}, u32[]{:S(2)}) copy-start(f32[4,2,1536]{2,1,0:T(2,128)} %get-tuple-element.55) | copy-start | bytes 147460
  137.4 9.3 %copy-start.1 = (f32[8,2,1536]{2,1,0:T(2,128)S(1)}, f32[8,2,1536]{2,1,0:T(2,128)}, u32[]{:S(2)}) copy-start(f32[8,2,1536]{2,1,0:T(2,128)} %get-tuple-element.56) | copy-start | bytes 294916
  147.4 9.3 %copy-start = (bf16[64,1536]{1,0:T(8,128)(2,1)S(1)}, bf16[64,1536]{1,0:T(8,128)(2,1)}, u32[]{:S(2)}) copy-start(bf16[64,1536]{1,0:T(8,128)(2,1)} %get-tuple-element.74) | copy-start | bytes 589828

commit v2 on v1

--- a/solution.py
+++ b/solution.py
@@ -14,6 +14,10 @@
 stable_eps = 1e-08
 weight_decay = 0.1
 LANES = 128
+PACKED = 16
+AHEAD = 2
+VMEM_MOMENTS = 40 * 2**20
+VMEM_ENCODE = 40 * 2**20
 
 
 def contract(left, right, left_dim, right_dim):
@@ -521,81 +525,6 @@
     )(inputs, cotangent, weight_in, weight_out)
 
 
-def exchange_kernel(plan, sizes, *refs):
-    count = len(plan)
-    sources, targets = refs[:count], refs[count : 2 * count]
-    send_sem, recv_sem, own_sem = refs[2 * count :]
-    axes = sorted(set(axis for axis, _ in plan))
-    me = {axis: lax.axis_index(axis) for axis in axes}
-    barrier = pltpu.get_barrier_semaphore()
-    greeted = 0
-    for axis in axes:
-        for step in range(1, sizes[axis]):
-            peer = lax.rem(me[axis] + step, sizes[axis])
-            pl.semaphore_signal(
-                barrier, inc=1, device_id={axis: peer}, device_id_type=pl.DeviceIdType.MESH
-            )
-            greeted += 1
-    owns = []
-    for item, (axis, scatter) in enumerate(plan):
-        block = sources[item].at[me[axis]] if scatter else sources[item]
-        own = pltpu.make_async_copy(block, targets[item].at[me[axis]], own_sem.at[item])
-        own.start()
-        owns.append(own)
-    pl.semaphore_wait(barrier, greeted)
-    copies = []
-    at = 0
-    for item, (axis, scatter) in enumerate(plan):
-        for step in range(1, sizes[axis]):
-            peer = lax.rem(me[axis] + step, sizes[axis])
-            block = sources[item].at[peer] if scatter else sources[item]
-            copy = pltpu.make_async_remote_copy(
-                src_ref=block,
-                dst_ref=targets[item].at[me[axis]],
-                send_sem=send_sem.at[at],
-                recv_sem=recv_sem.at[at],
-                device_id={axis: peer},
-                device_id_type=pl.DeviceIdType.MESH,
-            )
-            copy.start()
-            copies.append(copy)
-            at += 1
-    for own in owns:
-        own.wait()
-    for copy in copies:
-        copy.wait()
-
-
-def exchange(identity, plan, sizes, *arrays):
-    flights = sum(sizes[axis] - 1 for axis, _ in plan)
-    shapes = [
-        jax.ShapeDtypeStruct(
-            array.shape if scatter else (sizes[axis],) + array.shape, array.dtype
-        )
-        for array, (axis, scatter) in zip(arrays, plan)
-    ]
-    return pl.pallas_call(
-        functools.partial(exchange_kernel, plan, sizes),
-        out_shape=shapes,
-        in_specs=[pl.BlockSpec(memory_space=pl.ANY)] * len(plan),
-        out_specs=[pl.BlockSpec(memory_space=pl.ANY)] * len(plan),
-        scratch_shapes=[
-            pltpu.SemaphoreType.DMA((flights,)),
-            pltpu.SemaphoreType.DMA((flights,)),
-            pltpu.SemaphoreType.DMA((len(plan),)),
-        ],
-        compiler_params=pltpu.CompilerParams(collective_id=identity, has_side_effects=True),
-        name=f"exchange{identity}",
-    )(*arrays)
-
-
-def lane_fold(values, combine):
-    folded = values[:, :LANES]
-    for at in range(LANES, values.shape[1], LANES):
-        folded = combine(folded, values[:, at : at + LANES])
-    return folded
-
-
 def row_block(rows):
     return 256 if rows % 256 == 0 else 128
 
@@ -608,106 +537,359 @@
     return jnp.concatenate(pieces, axis=1)
 
 
+def lane_fold(values, combine):
+    top = values[:, :LANES]
+    for at in range(LANES, values.shape[1], LANES):
+        top = combine(top, values[:, at : at + LANES])
+    return top
+
+
+def sublane_fold(values, combine):
+    top = values[:PACKED]
+    for low in range(PACKED, values.shape[0], PACKED):
+        top = combine(top, values[low : low + PACKED])
+    return top
+
+
+second_gain = ((1.0 - second_decay) / second_decay) ** 0.5
+moment_gain = (1.0 - momentum_decay) / momentum_decay / second_gain
+root_gain = second_decay**0.5 / momentum_decay
+
+
+def moments_block(at, gain, left_ref, right_ref, sources, targets, row_ref, row_at, col_ref, turned):
+    weight_ref, moment_ref, second_ref = sources
+    new_moment_ref, new_second_ref = targets
+    block, width = turned.shape[0], weight_ref.shape[1]
+    rows = span(at * block, block)
+    turned[:, :] = left_ref[:, rows].T
+    tile = 256 if width % 256 == 0 else 128
+    row_tops = [None, None]
+    for low in range(0, width, tile):
+        take = slice(low, low + tile)
+        pulled = contract(turned[...], right_ref[:, take], 1, 0) * gain
+        moment = moment_ref[rows, take] + (pulled * moment_gain).astype(jnp.bfloat16)
+        second = second_ref[rows, take] + (pulled * pulled).astype(jnp.bfloat16)
+        wide = second.astype(jnp.float32)
+        root = wide * lax.rsqrt(wide)
+        step = moment.astype(jnp.float32) / (root * root_gain + stable_eps / momentum_decay)
+        decayed = weight_ref[rows, take] * jnp.bfloat16(weight_decay)
+        weight_ref[rows, take] = step.astype(jnp.bfloat16) + decayed
+        new_moment_ref[rows, take] = moment
+        new_second_ref[rows, take] = second
+        for which, value in enumerate((jnp.abs(moment), second)):
+            top = lane_fold(value, jnp.maximum)
+            row_tops[which] = top if low == 0 else jnp.maximum(row_tops[which], top)
+            col_ref[which, :, take] = jnp.maximum(
+                col_ref[which, :, take], sublane_fold(value, jnp.maximum)
+            )
+    for which in range(2):
+        row_ref[row_at + which : row_at + which + 1, rows] = to_lanes(
+            row_tops[which].astype(jnp.float32)
+        )
+
+
 def moments_kernel(
-    factor_ref, left_ref, right_ref, weight_ref, moment_ref, second_ref,
-    update_ref, new_moment_ref, new_second_ref, row_ref, col_ref,
+    factor_ref, inputs_hbm, delta_hbm, hidden_hbm, cotangent_hbm,
+    weight_in_hbm, moment_in_hbm, second_in_hbm, weight_out_hbm, moment_out_hbm, second_out_hbm,
+    update_in, update_out, new_moment_in, new_second_in, new_moment_out, new_second_out,
+    by_col, by_row,
+    inputs, delta, hidden, cotangent,
+    weight_in, moment_in, second_in, weight_out, moment_out, second_out,
+    cols_in, cols_out, turned_in, turned_out, side_sem, in_sem, out_sem, put_in, put_out,
 ):
-    gradient = contract(left_ref[...], right_ref[...], 0, 0)
-    scaled = gradient * factor_ref[0:1, 0:1]
-    moment_new = momentum_decay * moment_ref[...].astype(jnp.float32) + (
-        1.0 - momentum_decay
-    ) * scaled
-    second_new = second_decay * second_ref[...].astype(jnp.float32) + (
-        1.0 - second_decay
-    ) * scaled * scaled
-    update = moment_new / (jnp.sqrt(second_new) + stable_eps) + weight_decay * weight_ref[
-        ...
-    ].astype(jnp.float32)
-    update_ref[...] = update.astype(jnp.bfloat16)
-    new_moment_ref[...] = moment_new.astype(jnp.bfloat16)
-    new_second_ref[...] = second_new.astype(jnp.bfloat16)
-    size = jnp.abs(moment_new)
-    row_ref[0:1, :] = to_lanes(lane_fold(size, jnp.maximum))
-    row_ref[1:2, :] = to_lanes(lane_fold(second_new, jnp.maximum))
-
-    @pl.when(pl.program_id(0) == 0)
-    def _():
-        col_ref[...] = jnp.zeros_like(col_ref)
-
-    col_ref[0:1, :] = jnp.maximum(col_ref[0:1, :], jnp.max(size, axis=0, keepdims=True))
-    col_ref[1:2, :] = jnp.maximum(col_ref[1:2, :], jnp.max(second_new, axis=0, keepdims=True))
-
-
-def moments(factor, left, right, weight, moment, second):
-    rows, cols = weight.shape
-    tokens = left.shape[0]
-    block = row_block(rows)
-    tile = pl.BlockSpec((block, cols), lambda i: (i, 0))
-    half = jax.ShapeDtypeStruct((rows, cols), jnp.bfloat16)
+    block_in, block_out = turned_in.shape[0], turned_out.shape[0]
+    steps_in, steps_out = weight_in.shape[0] // block_in, weight_out.shape[0] // block_out
+    sides = [
+        pltpu.make_async_copy(source, target, side_sem.at[at])
+        for at, (source, target) in enumerate(
+            (
+                (inputs_hbm, inputs), (delta_hbm, delta),
+                (hidden_hbm, hidden), (cotangent_hbm, cotangent),
+            )
+        )
+    ]
+    pairs_in = (
+        (weight_in_hbm, weight_in), (moment_in_hbm, moment_in), (second_in_hbm, second_in)
+    )
+    pairs_out = (
+        (weight_out_hbm, weight_out), (moment_out_hbm, moment_out), (second_out_hbm, second_out)
+    )
+
+    def loads(pairs, sems, block, at):
+        rows = span(at * block, block)
+        return [
+            pltpu.make_async_copy(source.at[rows, :], target.at[rows, :], sems.at[which, at])
+            for which, (source, target) in enumerate(pairs)
+        ]
+
+    def begin_in(at):
+        for copy in loads(pairs_in, in_sem, block_in, at):
+            copy.start()
+
+    def begin_out(at):
+        for copy in loads(pairs_out, out_sem, block_out, at):
+            copy.start()
+
+    def put(source, target, sems, block, at):
+        rows = span(at * block, block)
+        return pltpu.make_async_copy(source.at[rows, :], target.at[rows, :], sems.at[at])
+
+    sides[0].start()
+    sides[1].start()
+    for at in range(AHEAD):
+        begin_in(at)
+    cols_in[...] = jnp.zeros_like(cols_in)
+    cols_out[...] = jnp.zeros_like(cols_out)
+    gain = factor_ref[0:1, 0:1] * second_gain
+    sides[0].wait()
+    sides[1].wait()
+    sides[2].start()
+    sides[3].start()
+
+    @pl.loop(0, steps_in)
+    def _(at):
+        pl.when(at + AHEAD < steps_in)(lambda: begin_in(at + AHEAD))
+        pl.when(at + AHEAD >= steps_in)(lambda: begin_out(at + AHEAD - steps_in))
+        for copy in loads(pairs_in, in_sem, block_in, at):
+            copy.wait()
+        moments_block(
+            at, gain, inputs, delta, (weight_in, moment_in, second_in),
+            (new_moment_in, new_second_in), by_col, 0, cols_in, turned_in,
+        )
+        put(weight_in, update_in, put_in, block_in, at).start()
+
+    sides[2].wait()
+    sides[3].wait()
+
+    @pl.loop(0, steps_out)
+    def _(at):
+        pl.when(at + AHEAD < steps_out)(lambda: begin_out(at + AHEAD))
+        for copy in loads(pairs_out, out_sem, block_out, at):
+            copy.wait()
+        moments_block(
+            at, gain, hidden, cotangent, (weight_out, moment_out, second_out),
+            (new_moment_out, new_second_out), by_row, 2, cols_out, turned_out,
+        )
+        put(weight_out, update_out, put_out, block_out, at).start()
+
+    for which in range(2):
+        top = cols_in[which].astype(jnp.float32)
+        by_row[which : which + 1, :] = jnp.max(top, axis=0, keepdims=True)
+        top = cols_out[which].astype(jnp.float32)
+        by_col[which + 2 : which + 3, :] = jnp.max(top, axis=0, keepdims=True)
+    for at in range(steps_in):
+        put(weight_in, update_in, put_in, block_in, at).wait()
+    for at in range(steps_out):
+        put(weight_out, update_out, put_out, block_out, at).wait()
+
+
+def held(shape):
+    return pltpu.VMEM(shape, jnp.bfloat16)
+
+
+def moments(factor, inputs, delta, hidden, cotangent, first, latter):
+    width, units = first[0].shape
+    tokens = inputs.shape[0]
+    block_in, block_out = row_block(width), row_block(units)
+    steps_in, steps_out = width // block_in, units // block_out
+    inside = pl.BlockSpec(memory_space=pltpu.VMEM)
+    anywhere = pl.BlockSpec(memory_space=pl.ANY)
     return pl.pallas_call(
         moments_kernel,
-        grid=(rows // block,),
         out_shape=[
-            half,
-            half,
-            half,
-            jax.ShapeDtypeStruct((2, rows), jnp.float32),
-            jax.ShapeDtypeStruct((2, cols), jnp.float32),
+            jax.ShapeDtypeStruct((width, units), jnp.bfloat16),
+            jax.ShapeDtypeStruct((units, width), jnp.bfloat16),
+            held((width, units)),
+            held((width, units)),
+            held((units, width)),
+            held((units, width)),
+            jax.ShapeDtypeStruct((4, width), jnp.float32),
+            jax.ShapeDtypeStruct((4, units), jnp.float32),
         ],
-        in_specs=[
-            pl.BlockSpec((8, LANES), lambda i: (0, 0)),
-            pl.BlockSpec((tokens, block), lambda i: (0, i)),
-            pl.BlockSpec((tokens, cols), lambda i: (0, 0)),
-            tile,
-            tile,
-            tile,
+        in_specs=[inside] + [anywhere] * 10,
+        out_specs=[anywhere] * 2 + [inside] * 6,
+        scratch_shapes=[
+            held((tokens, width)),
+            held((tokens, units)),
+            held((tokens, units)),
+            held((tokens, width)),
+        ]
+        + [held((width, units))] * 3
+        + [held((units, width))] * 3
+        + [
+            held((2, PACKED, units)),
+            held((2, PACKED, width)),
+            held((block_in, tokens)),
+            held((block_out, tokens)),
+            pltpu.SemaphoreType.DMA((4,)),
+            pltpu.SemaphoreType.DMA((3, steps_in)),
+            pltpu.SemaphoreType.DMA((3, steps_out)),
+            pltpu.SemaphoreType.DMA((steps_in,)),
+            pltpu.SemaphoreType.DMA((steps_out,)),
         ],
-        out_specs=[
-            tile,
-            tile,
-            tile,
-            pl.BlockSpec((2, block), lambda i: (0, i)),
-            pl.BlockSpec((2, cols), lambda i: (0, 0)),
+        compiler_params=pltpu.CompilerParams(vmem_limit_bytes=VMEM_MOMENTS),
+        name="moments",
+    )(factor, inputs, delta, hidden, cotangent, *first, *latter)
+
+
+def tops_kernel(sizes, col_ref, row_ref, all_col, all_row, send_c, recv_c, send_r, recv_r):
+    jobs = (
+        ("col", col_ref, all_col, send_c, recv_c),
+        ("row", row_ref, all_row, send_r, recv_r),
+    )
+    barrier = pltpu.get_barrier_semaphore()
+    for axis, *_ in jobs:
+        me = lax.axis_index(axis)
+        for off in range(1, sizes[axis]):
+            peer = lax.rem(me + off, sizes[axis])
+            pl.semaphore_signal(barrier, inc=1, device_id={axis: peer}, device_id_type=MESH)
+    pl.semaphore_wait(barrier, sizes["col"] + sizes["row"] - 2)
+    copies = []
+    for axis, source, target, send, receive in jobs:
+        me = lax.axis_index(axis)
+        for off in range(1, sizes[axis]):
+            peer = lax.rem(me + off, sizes[axis])
+            copy = remote(source, target.at[off], send.at[off], receive.at[off], axis, peer)
+            copy.start()
+            copies.append(copy)
+    for _, source, target, *_ in jobs:
+        target[0] = source[...]
+    for copy in copies:
+        copy.wait()
+
+
+def exchange_tops(sizes, by_col, by_row):
+    rows, cols = sizes["row"], sizes["col"]
+    inside = pl.BlockSpec(memory_space=pltpu.VMEM)
+    return pl.pallas_call(
+        functools.partial(tops_kernel, sizes),
+        out_shape=[
+            jax.ShapeDtypeStruct((cols,) + by_col.shape, jnp.float32),
+            jax.ShapeDtypeStruct((rows,) + by_row.shape, jnp.float32),
         ],
-        name="moments",
-    )(factor, left, right, weight, moment, second)
-
-
-def encode_kernel(moment_ref, second_ref, row_ref, col_ref, code_moment_ref, code_second_ref):
-    rows, cols = moment_ref.shape
-    for which, (source, target) in enumerate(
-        ((moment_ref, code_moment_ref), (second_ref, code_second_ref))
+        in_specs=[inside] * 2,
+        out_specs=[inside] * 2,
+        scratch_shapes=[
+            pltpu.SemaphoreType.DMA((cols,)),
+            pltpu.SemaphoreType.DMA((cols,)),
+            pltpu.SemaphoreType.DMA((rows,)),
+            pltpu.SemaphoreType.DMA((rows,)),
+        ],
+        compiler_params=pltpu.CompilerParams(
+            collective_id=1, has_side_effects=True, vmem_limit_bytes=4 * 2**20
+        ),
+        name="tops",
+    )(by_col, by_row)
+
+
+def encode_block(at, block, sources, targets, row_ref, row_at, col_ref, col_at):
+    cols = targets[0].shape[1]
+    for which in range(2):
+        source, target = sources[which], targets[which]
+        for low in range(0, block, LANES):
+            rows = span(at * block + low, LANES)
+            inverse = row_ref[row_at + which : row_at + which + 1, rows]
+            inverse = jnp.broadcast_to(inverse, (LANES, LANES)).T
+            for lane in range(0, cols, LANES):
+                other = col_ref[col_at + which : col_at + which + 1, lane : lane + LANES]
+                value = source[rows, lane : lane + LANES].astype(jnp.float32)
+                value = value * jnp.maximum(inverse, other)
+                target[rows, lane : lane + LANES] = value.astype(jnp.bfloat16)
+
+
+def encode_kernel(
+    all_col, all_row, moment_in, second_in, moment_out, second_out,
+    code_moment_in, code_second_in, code_moment_out, code_second_out,
+    row_scale_in, col_scale_in, row_scale_out, col_scale_out,
+    inverse_col, inverse_row, made_moment_in, made_second_in, made_moment_out, made_second_out,
+    in_sem, out_sem,
+):
+    for source, inverse, scales in (
+        (all_col, inverse_col, (row_scale_in, col_scale_out)),
+        (all_row, inverse_row, (col_scale_in, row_scale_out)),
     ):
-        for low in range(0, rows, LANES):
-            span = pl.ds(low, LANES)
-            inverse = 1.0 / row_ref[which : which + 1, low : low + LANES]
-            inverse = jnp.broadcast_to(inverse, (LANES, LANES)).T
-            for at in range(0, cols, LANES):
-                other = 1.0 / col_ref[which : which + 1, at : at + LANES]
-                value = source[span, at : at + LANES].astype(jnp.float32)
-                target[span, at : at + LANES] = (value * jnp.maximum(inverse, other)).astype(
-                    jnp.bfloat16
-                )
-
-
-def encode(moment, second, row_top, col_top):
-    rows, cols = moment.shape
-    block = row_block(rows)
-    tile = pl.BlockSpec((block, cols), lambda i: (i, 0))
-    half = jax.ShapeDtypeStruct((rows, cols), jnp.bfloat16)
+        top = source[0]
+        for at in range(1, source.shape[0]):
+            top = jnp.maximum(top, source[at])
+        for at in range(4):
+            decay = second_decay if at % 2 else momentum_decay
+            scale = jnp.maximum(top[at : at + 1] * decay, 1.0)
+            scales[at // 2][at % 2 : at % 2 + 1, :] = scale
+            inverse[at : at + 1, :] = decay / scale
+
+    jobs = (
+        (
+            (moment_in, second_in), (made_moment_in, made_second_in),
+            (code_moment_in, code_second_in), inverse_col, 0, inverse_row, 0, in_sem,
+        ),
+        (
+            (moment_out, second_out), (made_moment_out, made_second_out),
+            (code_moment_out, code_second_out), inverse_row, 2, inverse_col, 2, out_sem,
+        ),
+    )
+
+    def puts(made, codes, sems, block, at):
+        rows = span(at * block, block)
+        return [
+            pltpu.make_async_copy(made[i].at[rows, :], codes[i].at[rows, :], sems.at[i, at])
+            for i in range(2)
+        ]
+
+    for sources, made, codes, row_ref, row_at, col_ref, col_at, sems in jobs:
+        block = row_block(made[0].shape[0])
+
+        @pl.loop(0, made[0].shape[0] // block)
+        def _(at):
+            encode_block(at, block, sources, made, row_ref, row_at, col_ref, col_at)
+            for copy in puts(made, codes, sems, block, at):
+                copy.start()
+
+    for sources, made, codes, row_ref, row_at, col_ref, col_at, sems in jobs:
+        block = row_block(made[0].shape[0])
+        for at in range(made[0].shape[0] // block):
+            for copy in puts(made, codes, sems, block, at):
+                copy.wait()
+
+
+def encode(all_col, all_row, moment_in, second_in, moment_out, second_out):
+    width, units = moment_in.shape
+    inside = pl.BlockSpec(memory_space=pltpu.VMEM)
+    anywhere = pl.BlockSpec(memory_space=pl.ANY)
+    half, full = jnp.bfloat16, jnp.float32
     return pl.pallas_call(
         encode_kernel,
-        grid=(rows // block,),
-        out_shape=[half, half],
-        in_specs=[
-            tile,
-            tile,
-            pl.BlockSpec((2, block), lambda i: (0, i)),
-            pl.BlockSpec((2, cols), lambda i: (0, 0)),
+        out_shape=[
+            jax.ShapeDtypeStruct((width, units), half),
+            jax.ShapeDtypeStruct((width, units), half),
+            jax.ShapeDtypeStruct((units, width), half),
+            jax.ShapeDtypeStruct((units, width), half),
+            jax.ShapeDtypeStruct((2, width), full),
+            jax.ShapeDtypeStruct((2, units), full),
+            jax.ShapeDtypeStruct((2, units), full),
+            jax.ShapeDtypeStruct((2, width), full),
         ],
-        out_specs=[tile, tile],
+        in_specs=[inside] * 6,
+        out_specs=[anywhere] * 4 + [inside] * 4,
+        scratch_shapes=[
+            pltpu.VMEM((4, width), full),
+            pltpu.VMEM((4, units), full),
+            pltpu.VMEM((width, units), half),
+            pltpu.VMEM((width, units), half),
+            pltpu.VMEM((units, width), half),
+            pltpu.VMEM((units, width), half),
+            pltpu.SemaphoreType.DMA((2, width // row_block(width))),
+            pltpu.SemaphoreType.DMA((2, units // row_block(units))),
+        ],
+        compiler_params=pltpu.CompilerParams(vmem_limit_bytes=VMEM_ENCODE),
         name="encode",
-    )(moment, second, row_top, col_top)
+    )(
+        all_col,
+        all_row,
+        *(
+            pltpu.with_memory_space_constraint(value, pltpu.VMEM)
+            for value in (moment_in, second_in, moment_out, second_out)
+        ),
+    )
 
 
 def shards(
@@ -716,26 +898,20 @@
     all_inputs, all_cotangent, all_hidden, all_delta, input_grad, factor = front(
         sizes, inputs, cotangent, weight_in, weight_out
     )
-    update_in, moment_new_in, second_new_in, rows_in, cols_in = moments(
-        factor, all_inputs, all_delta, weight_in, moment_in, second_in
-    )
-    update_out, moment_new_out, second_new_out, rows_out, cols_out = moments(
-        factor, all_hidden, all_cotangent, weight_out, moment_out, second_out
-    )
-    rows_in, cols_out, cols_in, rows_out = exchange(
-        5,
-        (("col", False), ("col", False), ("row", False), ("row", False)),
-        sizes,
-        rows_in,
-        cols_out,
-        cols_in,
-        rows_out,
-    )
-    rows_in, cols_out, cols_in, rows_out = (
-        jnp.maximum(jnp.max(tops, axis=0), 1.0) for tops in (rows_in, cols_out, cols_in, rows_out)
-    )
-    code_moment_in, code_second_in = encode(moment_new_in, second_new_in, rows_in, cols_in)
-    code_moment_out, code_second_out = encode(moment_new_out, second_new_out, rows_out, cols_out)
+    update_in, update_out, *kept, by_col, by_row = moments(
+        factor,
+        all_inputs,
+        all_delta,
+        all_hidden,
+        all_cotangent,
+        (weight_in, moment_in, second_in),
+        (weight_out, moment_out, second_out),
+    )
+    all_col, all_row = exchange_tops(sizes, by_col, by_row)
+    (
+        code_moment_in, code_second_in, code_moment_out, code_second_out,
+        rows_in, cols_in, rows_out, cols_out,
+    ) = encode(all_col, all_row, *kept)
     return (
         input_grad,
         update_in,

time: 158 us -> 137 us (0.87)
  Pallas kernels: 153 us -> 132 us
  other arithmetic: 3.06 us -> 0 us
  local copies, waits for them, and re-layouts: 0.69 us -> 3.46 us
    pallas_call x5 -> x3, Pallas kernels: 61.7 us -> 40.9 us  [the longest x1 23.3 us: moments(): pl.pallas_call(moments_kernel, out_shape=[jax.ShapeDtypeStruct((width, un...]
    unnamed x7 -> x11, local copies, waits for them, and re-layouts: 0.69 us -> 3.46 us
    reduce_max x4 -> x0, other arithmetic: 1.83 us -> none  [shards(): jnp.max(tops, axis=0)]
where the time goes in v2:
time: 137 us; the launch traced here: 136 us
  Pallas kernels  132 us (96%)
  local copies, waits for them, and re-layouts  3.46 us (3%)
    pallas_call x1, Pallas kernels, front(): pl.pallas_call(kernel, out_shape=[jax.ShapeDtypeStruct((tokens, width), b...  91.2 us
    pallas_call x1, Pallas kernels, moments(): pl.pallas_call(moments_kernel, out_shape=[jax.ShapeDtypeStruct((width, un...  23.3 us
    pallas_call x1, Pallas kernels, encode(): pl.pallas_call(encode_kernel, out_shape=[jax.ShapeDtypeStruct((width, uni...  9.11 us
    pallas_call x1, Pallas kernels, exchange_tops(): pl.pallas_call(functools.partial(tops_kernel, sizes), out_shape=[jax.Shap...  8.47 us
    unnamed x11, local copies, waits for them, and re-layouts  3.46 us

profile of v2, /device:TPU:0, one launch (start us, length us, event | category | flops | bytes accessed | tf_op | source)
XLA Modules:
  0.0 136.3 jit_solution(1312703374663474000)
XLA Ops:
  0.6 91.2 %front.1 = (bf16[512,1536]{1,0:T(8,128)(2,1)}, bf16[512,1536]{1,0:T(8,128)(2,1)}, bf16[512,1536]{1,0:T(8,128)(2,1)}, bf16[512,1536]{1,0:T(8,128)(2,1)}, bf16[64,1536]{1,0:T(8,128)(2,1)}, /*index=5*/f32[8,128]{1,0:T(8,128)}) custom-call(bf16[64,1536]{1,0:T(8,128)(2,1)} %refs_0_.1, bf16[64,1536]{1,0:T(8,128)(2,1)} %refs_1_.1, ...), custom_call_target="tpu_custom_call" | custom-call | tf_op jit(solution)/shard_map/front/pallas_call | solution.py:508
  91.9 23.3 %moments.1 = (bf16[1536,1536]{1,0:T(8,128)(2,1)}, bf16[1536,1536]{1,0:T(8,128)(2,1)}, bf16[1536,1536]{1,0:T(8,128)(2,1)S(1)}, bf16[1536,1536]{1,0:T(8,128)(2,1)S...) custom-call(f32[8,128]{1,0:T(8,128)} %get-tuple-element.36.factor_re, ...), custom_call_target="tpu_custom_call" | custom-call | tf_op jit(solution)/shard_map/moments/pallas_call | solution.py:697
  115.2 0.0 copy-start.2
  115.2 0.7 copy-done.2
  115.9 0.0 copy-start.3
  115.9 0.7 copy-done.3
  116.7 8.5 %tops.1 = (f32[8,4,1536]{2,1,0:T(4,128)S(1)}, f32[4,4,1536]{2,1,0:T(4,128)S(1)}) custom-call(f32[4,1536]{1,0:T(4,128)S(1)} %copy-done.2, f32[4,1536]{1,0:T(4,128)S(1)} %copy-done.3), custom_call_target="tpu_custom_call" | custom-call | tf_op jit(solution)/shard_map/tops/pallas_call | solution.py:764
  125.2 0.0 copy-start
  125.2 0.7 copy-done
  125.8 0.0 copy-start.1
  125.8 0.6 copy-done.1
  126.5 0.0 copy-start.4
  126.5 9.1 %encode.1 = (bf16[1536,1536]{1,0:T(8,128)(2,1)}, bf16[1536,1536]{1,0:T(8,128)(2,1)}, bf16[1536,1536]{1,0:T(8,128)(2,1)}, bf16[1536,1536]{1,0:T(8,128)(2,1)}, f32...) custom-call(f32[8,4,1536]{2,1,0:T(4,128)} %copy-done, f32[4,4,1536]{2,1,0:T(4,128)} %copy-done.1, ...), custom_call_target="tpu_custom_call" | custom-call | tf_op jit(solution)/shard_map/encode/pallas_call | solution.py:859
  135.6 0.0 copy-done.4
  135.6 0.7 copy.20
Async XLA Ops:
  115.2 0.7 copy-start.2
  115.9 0.7 copy-start.3
  125.2 0.7 copy-start
  125.8 0.6 copy-start.1
  126.5 9.1 %copy-start.4 = (bf16[64,1536]{1,0:T(8,128)(2,1)S(1)}, bf16[64,1536]{1,0:T(8,128)(2,1)}, u32[]{:S(2)}) copy-start(bf16[64,1536]{1,0:T(8,128)(2,1)} %get-tuple-element.70) | copy-start | bytes 589828

commit v3 on v2

--- a/solution.py
+++ b/solution.py
@@ -77,7 +77,7 @@
     t, width = x_ref.shape
     hidden = wi.shape[1]
     size = ny * t
-    half = size // 2
+    half = t // 2
     piece = half // nx
     tokens = size * nz
     r, k = lax.axis_index("row"), lax.axis_index("col")
@@ -165,6 +165,10 @@
             pl.when(there)(lambda i=item: z_copy(i, zs, g, 0, sign).start())
             y_copies(item, zs, g)
 
+    def first_row(unit):
+        g, j = unit
+        return (order[g][0] * ny + lax.rem(y + j, ny)) * t
+
     def y_wait(g, item):
         zs, _ = order[g]
         for off in range(1, ny):
@@ -175,13 +179,14 @@
             ).wait_recv()
 
     tile_h, tile_w = lane_tile(hidden), lane_tile(width)
-
-    def forward_product(g, item):
-        first = order[g][0] * size
+    chunks = width // tile_w
+
+    def forward_product(units, item):
         left = jnp.concatenate(
             [
-                acts[item, span(first + (1 - core) * half, half), :],
-                acts[item, span(first + core * half, half), :],
+                acts[item, span(first_row(unit) + which * half, half), :]
+                for unit in units
+                for which in (1 - core, core)
             ],
             axis=0,
         )
@@ -193,135 +198,132 @@
                 part = contract(left, wi[:, at], 1, 0)
             else:
                 part = contract(left, wo[at, :], 1, 1)
-            pair_send[g, item, :, at] = part[:half]
-            pair_own[g, item, :, at] = part[half:]
-
-        pair_copy(g, item).start()
-        pending.append(pair_copy(g, item))
-
-    def pair_copy(g, item):
+            for i, (g, j) in enumerate(units):
+                low = i * t
+                pair_send[g, j, item, :, at] = part[low : low + half]
+                pair_own[g, j, item, :, at] = part[low + half : low + t]
+
+        for unit in units:
+            pair_copy(unit, item).start()
+            pending.append(pair_copy(unit, item))
+
+    def pair_copy(unit, item):
+        g, j = unit
         return remote(
-            pair_send.at[g, item], pair_recv.at[g, item],
-            pair_s.at[g, item], pair_r.at[g, item], "row", partner,
-        )
-
-    def line_copy(g, off):
+            pair_send.at[g, j, item], pair_recv.at[g, j, item],
+            pair_s.at[item, g, j], pair_r.at[item, g, j], "row", partner,
+        )
+
+    def line_copy(unit, off):
+        g, j = unit
         return remote(
-            line_send.at[g, off - 1], line_recv.at[g, off - 1],
-            line_s.at[g, off], line_r.at[g, off], "row", line_peer(off),
-        )
-
-    def pair_sum(g):
+            line_send.at[g, j, off - 1], line_recv.at[g, j, off - 1],
+            line_s.at[g, j, off], line_r.at[g, j, off], "row", line_peer(off),
+        )
+
+    def pair_sum(unit):
+        g, j = unit
         for item in range(2):
-            pair_copy(g, item).wait_recv()
+            pair_copy(unit, item).wait_recv()
         for off in range(1, nx):
             take = span(lax.rem(x + off, nx) * piece, piece)
             for item in range(2):
-                line_send[g, off - 1, item] = (
-                    pair_own[g, item, take, :] + pair_recv[g, item, take, :]
+                line_send[g, j, off - 1, item] = (
+                    pair_own[g, j, item, take, :] + pair_recv[g, j, item, take, :]
                 ).astype(jnp.bfloat16)
-            line_copy(g, off).start()
-            pending.append(line_copy(g, off))
+            line_copy(unit, off).start()
+            pending.append(line_copy(unit, off))
         take = span(x * piece, piece)
         for item in range(2):
-            line_own[g, item] = pair_own[g, item, take, :] + pair_recv[g, item, take, :]
-
-    def gather_block(g, xs):
-        return hd.at[:, span(order[g][0] * size + core * half + xs * piece, piece), :]
-
-    def gather_copy(g, off):
-        block = gather_block(g, x)
+            line_own[g, j, item] = pair_own[g, j, item, take, :] + pair_recv[g, j, item, take, :]
+
+    def gather_block(unit, xs):
+        return hd.at[:, span(first_row(unit) + core * half + xs * piece, piece), :]
+
+    def gather_copy(unit, off):
+        g, j = unit
+        block = gather_block(unit, x)
         return remote(
-            block, block, gather_s.at[g, off], gather_r.at[g, off], "row", line_peer(off)
-        )
-
-    def active(g):
+            block, block, gather_s.at[g, j, off], gather_r.at[g, j, off], "row", line_peer(off)
+        )
+
+    def active(unit):
+        g, j = unit
         for off in range(1, nx):
-            line_copy(g, off).wait_recv()
-        first = order[g][0] * size + core * half + x * piece
+            line_copy(unit, off).wait_recv()
+        first = first_row(unit) + core * half + x * piece
 
         @pl.loop(0, hidden // LANES)
         def _(n):
             at = span(n * LANES, LANES)
-            preact, hidden_grad = line_own[g, 0, :, at], line_own[g, 1, :, at]
+            preact, hidden_grad = line_own[g, j, 0, :, at], line_own[g, j, 1, :, at]
             for off in range(1, nx):
-                preact = preact + line_recv[g, off - 1, 0, :, at].astype(jnp.float32)
-                hidden_grad = hidden_grad + line_recv[g, off - 1, 1, :, at].astype(jnp.float32)
+                preact = preact + line_recv[g, j, off - 1, 0, :, at].astype(jnp.float32)
+                hidden_grad = hidden_grad + line_recv[g, j, off - 1, 1, :, at].astype(jnp.float32)
             value, slope = activate(preact, hidden_grad)
             hd[0, span(first, piece), at] = value
             hd[1, span(first, piece), at] = slope
 
         for off in range(1, nx):
-            gather_copy(g, off).start()
-            pending.append(gather_copy(g, off))
-
-    def share_copy(g, which):
-        block = hd.at[:, span(order[g][0] * size + which * half, half), :]
-        return remote(block, block, share_s.at[g], share_r.at[g], "row", partner)
-
-    def share(g):
+            gather_copy(unit, off).start()
+            pending.append(gather_copy(unit, off))
+
+    def share_copy(unit, which):
+        block = hd.at[:, span(first_row(unit) + which * half, half), :]
+        return remote(block, block, share_s.at[unit], share_r.at[unit], "row", partner)
+
+    def share(unit):
+        g, j = unit
         for off in range(1, nx):
-            xs = lax.rem(x + nx - off, nx)
-            block = gather_block(g, xs)
+            block = gather_block(unit, lax.rem(x + nx - off, nx))
             remote(
-                block, block, gather_s.at[g, off], gather_r.at[g, off], "row", line_peer(off)
+                block, block, gather_s.at[g, j, off], gather_r.at[g, j, off],
+                "row", line_peer(off),
             ).wait_recv()
-        share_copy(g, core).start()
-        pending.append(share_copy(g, core))
-
-    def share_wait(g):
-        share_copy(g, 1 - core).wait_recv()
-
-    def dx_copy(g, off):
+        share_copy(unit, core).start()
+        pending.append(share_copy(unit, core))
+
+    def share_wait(unit):
+        share_copy(unit, 1 - core).wait_recv()
+
+    def dx_copy(g, off, chunk):
         return remote(
-            dx_send.at[g, off - 1], dx_recv.at[g, off - 1],
-            dy_s.at[g, off], dy_r.at[g, off], "col", y_peer(off),
-        )
-
-    def back_product(groups):
-        left = jnp.concatenate(
-            [
-                hd[1, span(order[g][0] * size + lax.rem(y + off, ny) * t, t), :]
-                for g in groups
-                for off in range(ny)
-            ],
-            axis=0,
-        )
-
-        @pl.loop(0, width // tile_w)
-        def _(n):
-            at = span(n * tile_w, tile_w)
-            part = contract(left, wi[at, :], 1, 1)
-            for i, g in enumerate(groups):
-                for off in range(ny):
-                    low = (i * ny + off) * t
-                    if off == 0:
-                        dx_own[g, :, at] = part[low : low + t]
-                    else:
-                        dx_send[g, off - 1, :, at] = part[low : low + t].astype(jnp.bfloat16)
-
-        for g in groups:
+            dx_send.at[g, off - 1, chunk], dx_recv.at[g, off - 1, chunk],
+            dy_s.at[g, off, chunk], dy_r.at[g, off, chunk], "col", y_peer(off),
+        )
+
+    def back_product(batches):
+        units = [unit for at in batches for unit in groups[at]]
+        left = jnp.concatenate([hd[1, span(first_row(unit), t), :] for unit in units], axis=0)
+        for chunk in range(chunks):
+            part = contract(left, wi[chunk * tile_w : (chunk + 1) * tile_w, :], 1, 1)
+            for i, (g, j) in enumerate(units):
+                rows_of = part[i * t : (i + 1) * t]
+                if j == 0:
+                    dx_own[g, chunk] = rows_of
+                else:
+                    dx_send[g, j - 1, chunk] = rows_of.astype(jnp.bfloat16)
+                    dx_copy(g, j, chunk).start()
+                    pending.append(dx_copy(g, j, chunk))
+
+    def dz_copy(g, chunk):
+        return remote(
+            dz_send.at[g, chunk], dz_recv.at[z, chunk], dz_s.at[g, chunk], dz_r.at[z, chunk],
+            "col", order[g][0] * ny + y,
+        )
+
+    def back_sum(g):
+        for chunk in range(chunks):
+            total = dx_own[g, chunk]
             for off in range(1, ny):
-                dx_copy(g, off).start()
-                pending.append(dx_copy(g, off))
-
-    def dz_copy(g):
-        return remote(
-            dz_send.at[g], dz_recv.at[z], dz_s.at[g], dz_r.at[z], "col", order[g][0] * ny + y
-        )
-
-    def back_sum(g):
-        for off in range(1, ny):
-            dx_copy(g, off).wait_recv()
-        total = dx_own[g]
-        for off in range(1, ny):
-            total = total + dx_recv[g, off - 1].astype(jnp.float32)
-        if g == 0:
-            dx_own[0] = total
-        else:
-            dz_send[g] = total.astype(jnp.bfloat16)
-            dz_copy(g).start()
-            pending.append(dz_copy(g))
+                dx_copy(g, off, chunk).wait_recv()
+                total = total + dx_recv[g, off - 1, chunk].astype(jnp.float32)
+            if g == 0:
+                dx_own[0, chunk] = total
+            else:
+                dz_send[g, chunk] = total.astype(jnp.bfloat16)
+                dz_copy(g, chunk).start()
+                pending.append(dz_copy(g, chunk))
 
     outs = []
 
@@ -360,41 +362,51 @@
                     part = contract(left[:, at], right[...], 0, 0)
                     part_ref[...] += folded(part * part)
 
-    for s in range(nz + 3):
-        if s + 1 < nz:
-            forward(s + 1)
-        if s < nz:
+    others = range(1, ny)
+    groups = [[(0, 0)]]
+    groups += [[(g - 1, j) for j in others] + [(g, 0)] for g in range(1, nz)]
+    groups += [[(nz - 1, j) for j in others]]
+
+    for s in range(nz + 4):
+        if 1 <= s < nz:
+            forward(s)
+        if s <= nz:
             for item in range(2):
-                y_wait(s, item)
-                if s == 0:
+                if s >= 1:
+                    y_wait(s - 1, item)
+                else:
                     loads[2 + item].wait()
-                forward_product(s, item)
-        if 0 <= s - 1 < nz:
-            active(s - 1)
-        if s == nz - 1:
+                forward_product(groups[s], item)
+        if s == nz:
             put(acts.at[0], x_out, 0)
             put(acts.at[1], c_out, 1)
-        if s < nz:
-            pair_sum(s)
-        if s == nz and use_grams:
+        if 0 <= s - 1 <= nz:
+            for unit in groups[s - 1]:
+                active(unit)
+        if s <= nz:
+            for unit in groups[s]:
+                pair_sum(unit)
+        if s == nz + 1 and use_grams:
             gram(0, acts, 0)
             gram(1, acts, 1)
-        if 0 <= s - 2 < nz:
-            share(s - 2)
-        if 0 <= s - 3 < nz:
-            share_wait(s - 3)
-        if s == nz - 1:
-            back_product(list(range(nz - 3)))
+        if 0 <= s - 2 <= nz:
+            for unit in groups[s - 2]:
+                share(unit)
+        if 0 <= s - 3 <= nz:
+            for unit in groups[s - 3]:
+                share_wait(unit)
         if s == nz:
-            back_product([nz - 3])
+            back_product(list(range(nz - 2)))
+        if s == nz + 1:
+            back_product([nz - 2])
             for g in range(nz - 3):
                 back_sum(g)
-        if s == nz + 1:
-            back_product([nz - 2])
+        if s == nz + 2:
+            back_product([nz - 1])
             back_sum(nz - 3)
     put(hd.at[0], hidden_out, 2)
     put(hd.at[1], delta_out, 3)
-    back_product([nz - 1])
+    back_product([nz])
     local_total()
 
     def col_copy(off):
@@ -431,14 +443,16 @@
     factor = 1.0 / jnp.maximum(jnp.sqrt(total / entries), 1.0)
     factor_ref[...] = jnp.broadcast_to(factor, factor_ref.shape)
 
-    total = dx_own[0]
-    for off in range(1, nz):
-        zs = lax.rem(z + off, nz)
-        remote(
-            dz_send.at[1], dz_recv.at[zs], dz_s.at[1], dz_r.at[zs], "col", y_peer(1)
-        ).wait_recv()
-        total = total + dz_recv[zs].astype(jnp.float32)
-    grad_ref[...] = total.astype(jnp.bfloat16)
+    for chunk in range(chunks):
+        total = dx_own[0, chunk]
+        for off in range(1, nz):
+            zs = lax.rem(z + off, nz)
+            remote(
+                dz_send.at[1, chunk], dz_recv.at[zs, chunk],
+                dz_s.at[1, chunk], dz_r.at[zs, chunk], "col", y_peer(1),
+            ).wait_recv()
+            total = total + dz_recv[zs, chunk].astype(jnp.float32)
+        grad_ref[:, chunk * tile_w : (chunk + 1) * tile_w] = total.astype(jnp.bfloat16)
 
     for item in range(2):
         for way, sign, there in ways:
@@ -461,8 +475,10 @@
     t, width = inputs.shape
     hidden = weight_in.shape[1]
     size = t * ny
-    half, tokens = size // 2, size * nz
+    half, tokens = t // 2, size * nz
     piece = half // nx
+    tile = lane_tile(width)
+    parts = (width // tile, t, tile)
     entries = 2.0 * width * rows * hidden * cols
     bf, f4 = jnp.bfloat16, jnp.float32
     use_grams = tokens <= hidden
@@ -471,27 +487,27 @@
         pltpu.VMEM((2, tokens, width), bf),
         pltpu.VMEM(weight_in.shape, bf),
         pltpu.VMEM(weight_out.shape, bf),
-        pltpu.VMEM((nz, 2, half, hidden), f4),
-        pltpu.VMEM((nz, 2, half, hidden), f4),
-        pltpu.VMEM((nz, 2, half, hidden), f4),
-        pltpu.VMEM((nz, nx - 1, 2, piece, hidden), bf),
-        pltpu.VMEM((nz, nx - 1, 2, piece, hidden), bf),
-        pltpu.VMEM((nz, 2, piece, hidden), f4),
+        pltpu.VMEM((nz, ny, 2, half, hidden), f4),
+        pltpu.VMEM((nz, ny, 2, half, hidden), f4),
+        pltpu.VMEM((nz, ny, 2, half, hidden), f4),
+        pltpu.VMEM((nz, ny, nx - 1, 2, piece, hidden), bf),
+        pltpu.VMEM((nz, ny, nx - 1, 2, piece, hidden), bf),
+        pltpu.VMEM((nz, ny, 2, piece, hidden), f4),
         pltpu.VMEM((2, tokens, hidden), bf),
-        pltpu.VMEM((nz, t, width), f4),
-        pltpu.VMEM((nz, ny - 1, t, width), bf),
-        pltpu.VMEM((nz, ny - 1, t, width), bf),
-        pltpu.VMEM((nz, t, width), bf),
-        pltpu.VMEM((nz, t, width), bf),
+        pltpu.VMEM((nz,) + parts, f4),
+        pltpu.VMEM((nz, ny - 1) + parts, bf),
+        pltpu.VMEM((nz, ny - 1) + parts, bf),
+        pltpu.VMEM((nz,) + parts, bf),
+        pltpu.VMEM((nz,) + parts, bf),
         pltpu.VMEM((8, LANES), f4),
         pltpu.VMEM((cols, 8, LANES), f4),
         pltpu.VMEM((rows, 8, LANES), f4),
         pltpu.VMEM((2, tokens, tokens), f4) if use_grams else None,
         dma(4),
         dma(2, nz, 2), dma(2, nz), dma(2, nz, ny), dma(2, nz, ny),
-        dma(nz, 2), dma(nz, 2), dma(nz, nx), dma(nz, nx),
-        dma(nz, nx), dma(nz, nx), dma(nz), dma(nz),
-        dma(nz, ny), dma(nz, ny), dma(nz), dma(nz),
+        dma(2, nz, ny), dma(2, nz, ny), dma(nz, ny, nx), dma(nz, ny, nx),
+        dma(nz, ny, nx), dma(nz, ny, nx), dma(nz, ny), dma(nz, ny),
+        dma(nz, ny, parts[0]), dma(nz, ny, parts[0]), dma(nz, parts[0]), dma(nz, parts[0]),
         dma(cols), dma(cols), dma(rows), dma(rows), dma(4),
     ]
     kept = [item for item in scratch if item is not None]
@@ -703,8 +719,8 @@
             held((width, units)),
             held((units, width)),
             held((units, width)),
-            jax.ShapeDtypeStruct((4, width), jnp.float32),
-            jax.ShapeDtypeStruct((4, units), jnp.float32),
+            pltpu.VMEM((4, width), jnp.float32),
+            pltpu.VMEM((4, units), jnp.float32),
         ],
         in_specs=[inside] + [anywhere] * 10,
         out_specs=[anywhere] * 2 + [inside] * 6,
@@ -764,8 +780,8 @@
     return pl.pallas_call(
         functools.partial(tops_kernel, sizes),
         out_shape=[
-            jax.ShapeDtypeStruct((cols,) + by_col.shape, jnp.float32),
-            jax.ShapeDtypeStruct((rows,) + by_row.shape, jnp.float32),
+            pltpu.VMEM((cols,) + by_col.shape, jnp.float32),
+            pltpu.VMEM((rows,) + by_row.shape, jnp.float32),
         ],
         in_specs=[inside] * 2,
         out_specs=[inside] * 2,
@@ -779,7 +795,7 @@
             collective_id=1, has_side_effects=True, vmem_limit_bytes=4 * 2**20
         ),
         name="tops",
-    )(by_col, by_row)
+    )(*(pltpu.with_memory_space_constraint(top, pltpu.VMEM) for top in (by_col, by_row)))
 
 
 def encode_block(at, block, sources, targets, row_ref, row_at, col_ref, col_at):
@@ -798,12 +814,15 @@
 
 
 def encode_kernel(
-    all_col, all_row, moment_in, second_in, moment_out, second_out,
+    all_col, all_row, moment_in, second_in, moment_out, second_out, grad_from,
     code_moment_in, code_second_in, code_moment_out, code_second_out,
-    row_scale_in, col_scale_in, row_scale_out, col_scale_out,
+    row_scale_in, col_scale_in, row_scale_out, col_scale_out, grad_to,
     inverse_col, inverse_row, made_moment_in, made_second_in, made_moment_out, made_second_out,
-    in_sem, out_sem,
+    grad, in_sem, out_sem, grad_sem,
 ):
+    fetch = pltpu.make_async_copy(grad_from, grad, grad_sem.at[0])
+    store = pltpu.make_async_copy(grad, grad_to, grad_sem.at[1])
+    fetch.start()
     for source, inverse, scales in (
         (all_col, inverse_col, (row_scale_in, col_scale_out)),
         (all_row, inverse_row, (col_scale_in, row_scale_out)),
@@ -844,6 +863,9 @@
             for copy in puts(made, codes, sems, block, at):
                 copy.start()
 
+    fetch.wait()
+    store.start()
+    store.wait()
     for sources, made, codes, row_ref, row_at, col_ref, col_at, sems in jobs:
         block = row_block(made[0].shape[0])
         for at in range(made[0].shape[0] // block):
@@ -851,7 +873,7 @@
                 copy.wait()
 
 
-def encode(all_col, all_row, moment_in, second_in, moment_out, second_out):
+def encode(all_col, all_row, moment_in, second_in, moment_out, second_out, input_grad):
     width, units = moment_in.shape
     inside = pl.BlockSpec(memory_space=pltpu.VMEM)
     anywhere = pl.BlockSpec(memory_space=pl.ANY)
@@ -867,9 +889,10 @@
             jax.ShapeDtypeStruct((2, units), full),
             jax.ShapeDtypeStruct((2, units), full),
             jax.ShapeDtypeStruct((2, width), full),
+            jax.ShapeDtypeStruct(input_grad.shape, half),
         ],
-        in_specs=[inside] * 6,
-        out_specs=[anywhere] * 4 + [inside] * 4,
+        in_specs=[inside] * 6 + [anywhere],
+        out_specs=[anywhere] * 4 + [inside] * 4 + [anywhere],
         scratch_shapes=[
             pltpu.VMEM((4, width), full),
             pltpu.VMEM((4, units), full),
@@ -877,18 +900,19 @@
             pltpu.VMEM((width, units), half),
             pltpu.VMEM((units, width), half),
             pltpu.VMEM((units, width), half),
+            pltpu.VMEM(input_grad.shape, half),
             pltpu.SemaphoreType.DMA((2, width // row_block(width))),
             pltpu.SemaphoreType.DMA((2, units // row_block(units))),
+            pltpu.SemaphoreType.DMA((2,)),
         ],
         compiler_params=pltpu.CompilerParams(vmem_limit_bytes=VMEM_ENCODE),
         name="encode",
     )(
-        all_col,
-        all_row,
         *(
             pltpu.with_memory_space_constraint(value, pltpu.VMEM)
-            for value in (moment_in, second_in, moment_out, second_out)
+            for value in (all_col, all_row, moment_in, second_in, moment_out, second_out)
         ),
+        input_grad,
     )
 
 
@@ -910,8 +934,8 @@
     all_col, all_row = exchange_tops(sizes, by_col, by_row)
     (
         code_moment_in, code_second_in, code_moment_out, code_second_out,
-        rows_in, cols_in, rows_out, cols_out,
-    ) = encode(all_col, all_row, *kept)
+        rows_in, cols_in, rows_out, cols_out, input_grad,
+    ) = encode(all_col, all_row, *kept, input_grad)
     return (
         input_grad,
         update_in,

time: 137 us -> 126 us (0.920)
  Pallas kernels: 132 us -> 125 us
  local copies, waits for them, and re-layouts: 3.46 us -> 0 us
    pallas_call x1, Pallas kernels: 91.2 us -> 84 us  [front(): pl.pallas_call(kernel, out_shape=[jax.ShapeDtypeStruct((tokens, width), b...]
    unnamed x11 -> x0, local copies, waits for them, and re-layouts: 3.46 us -> none
    pallas_call x1, Pallas kernels: 8.47 us -> 10.2 us  [exchange_tops(): pl.pallas_call(functools.partial(tops_kernel, sizes), out_shape=[pltpu.VM...]
where the time goes in v3:
time: 126 us
  Pallas kernels  125 us (99%)
    pallas_call x1, Pallas kernels, front(): pl.pallas_call(kernel, out_shape=[jax.ShapeDtypeStruct((tokens, width), b...  84 us
    pallas_call x1, Pallas kernels, moments(): pl.pallas_call(moments_kernel, out_shape=[jax.ShapeDtypeStruct((width, un...  22.7 us
    pallas_call x1, Pallas kernels, exchange_tops(): pl.pallas_call(functools.partial(tops_kernel, sizes), out_shape=[pltpu.VM...  10.2 us
    pallas_call x1, Pallas kernels, encode(): pl.pallas_call(encode_kernel, out_shape=[jax.ShapeDtypeStruct((width, uni...  8.18 us

profile of v3, /device:TPU:0, one launch (start us, length us, event | category | flops | bytes accessed | tf_op | source)
XLA Modules:
  0.0 125.7 jit_solution(6094868404194419466)
XLA Ops:
  0.6 84.0 %front.1 = (bf16[512,1536]{1,0:T(8,128)(2,1)}, bf16[512,1536]{1,0:T(8,128)(2,1)}, bf16[512,1536]{1,0:T(8,128)(2,1)}, bf16[512,1536]{1,0:T(8,128)(2,1)}, bf16[64,1536]{1,0:T(8,128)(2,1)}, /*index=5*/f32[8,128]{1,0:T(8,128)}) custom-call(bf16[64,1536]{1,0:T(8,128)(2,1)} %refs_0_.1, bf16[64,1536]{1,0:T(8,128)(2,1)} %refs_1_.1, ...), custom_call_target="tpu_custom_call" | custom-call | tf_op jit(solution)/shard_map/front/pallas_call | solution.py:524
  84.7 22.7 %moments.1 = (bf16[1536,1536]{1,0:T(8,128)(2,1)}, bf16[1536,1536]{1,0:T(8,128)(2,1)}, bf16[1536,1536]{1,0:T(8,128)(2,1)S(1)}, bf16[1536,1536]{1,0:T(8,128)(2,1)S...) custom-call(f32[8,128]{1,0:T(8,128)} %get-tuple-element.36.factor_re, ...), custom_call_target="tpu_custom_call" | custom-call | tf_op jit(solution)/shard_map/moments/pallas_call | solution.py:713
  107.4 10.2 %tops.1 = (f32[8,4,1536]{2,1,0:T(4,128)S(1)}, f32[4,4,1536]{2,1,0:T(4,128)S(1)}) custom-call(f32[4,1536]{1,0:T(4,128)S(1)} %get-tuple-element.41.col_ref, f32[4,1536]{1,0:T(4,128)S(1)} %get-tuple-element.42.row_ref), custom_call_target="tpu_custom_call" | custom-call | tf_op jit(solution)/shard_map/tops/pallas_call | solution.py:780
  117.5 8.2 %encode.1 = (bf16[1536,1536]{1,0:T(8,128)(2,1)}, bf16[1536,1536]{1,0:T(8,128)(2,1)}, bf16[1536,1536]{1,0:T(8,128)(2,1)}, bf16[1536,1536]{1,0:T(8,128)(2,1)}, f32...) custom-call(f32[8,4,1536]{2,1,0:T(4,128)S(1)} %get-tuple-element.43., ...), custom_call_target="tpu_custom_call" | custom-call | tf_op jit(solution)/shard_map/encode/pallas_call | solution.py:881

commit v4 on v3

--- a/solution.py
+++ b/solution.py
@@ -253,9 +253,9 @@
             line_copy(unit, off).wait_recv()
         first = first_row(unit) + core * half + x * piece
 
-        @pl.loop(0, hidden // LANES)
+        @pl.loop(0, hidden // tile_h)
         def _(n):
-            at = span(n * LANES, LANES)
+            at = span(n * tile_h, tile_h)
             preact, hidden_grad = line_own[g, j, 0, :, at], line_own[g, j, 1, :, at]
             for off in range(1, nx):
                 preact = preact + line_recv[g, j, off - 1, 0, :, at].astype(jnp.float32)
@@ -386,9 +386,6 @@
         if s <= nz:
             for unit in groups[s]:
                 pair_sum(unit)
-        if s == nz + 1 and use_grams:
-            gram(0, acts, 0)
-            gram(1, acts, 1)
         if 0 <= s - 2 <= nz:
             for unit in groups[s - 2]:
                 share(unit)
@@ -397,6 +394,9 @@
                 share_wait(unit)
         if s == nz:
             back_product(list(range(nz - 2)))
+            if use_grams:
+                gram(0, acts, 0)
+                gram(1, acts, 1)
         if s == nz + 1:
             back_product([nz - 2])
             for g in range(nz - 3):
@@ -407,6 +407,7 @@
     put(hd.at[0], hidden_out, 2)
     put(hd.at[1], delta_out, 3)
     back_product([nz])
+    back_sum(nz - 2)
     local_total()
 
     def col_copy(off):
@@ -424,7 +425,6 @@
     for off in range(1, cols):
         col_copy(off).start()
         pending.append(col_copy(off))
-    back_sum(nz - 2)
     back_sum(nz - 1)
     for off in range(1, cols):
         col_copy(off).wait_recv()
@@ -652,18 +652,19 @@
 
     sides[0].start()
     sides[1].start()
-    for at in range(AHEAD):
-        begin_in(at)
+    begin_in(0)
     cols_in[...] = jnp.zeros_like(cols_in)
     cols_out[...] = jnp.zeros_like(cols_out)
     gain = factor_ref[0:1, 0:1] * second_gain
     sides[0].wait()
     sides[1].wait()
-    sides[2].start()
-    sides[3].start()
+    for at in range(1, AHEAD):
+        begin_in(at)
 
     @pl.loop(0, steps_in)
     def _(at):
+        pl.when(at == min(1, steps_in - 1))(sides[2].start)
+        pl.when(at == min(2, steps_in - 1))(sides[3].start)
         pl.when(at + AHEAD < steps_in)(lambda: begin_in(at + AHEAD))
         pl.when(at + AHEAD >= steps_in)(lambda: begin_out(at + AHEAD - steps_in))
         for copy in loads(pairs_in, in_sem, block_in, at):

time: 126 us -> 122 us (0.968)
  Pallas kernels: 125 us -> 121 us
    pallas_call x1, Pallas kernels: 84 us -> 81.7 us  [front(): pl.pallas_call(kernel, out_shape=[jax.ShapeDtypeStruct((tokens, width), b...]
where the time goes in v4:
time: 122 us
  Pallas kernels  121 us (99%)
    pallas_call x1, Pallas kernels, front(): pl.pallas_call(kernel, out_shape=[jax.ShapeDtypeStruct((tokens, width), b...  81.7 us
    pallas_call x1, Pallas kernels, moments(): pl.pallas_call(moments_kernel, out_shape=[jax.ShapeDtypeStruct((width, un...  22 us
    pallas_call x1, Pallas kernels, exchange_tops(): pl.pallas_call(functools.partial(tops_kernel, sizes), out_shape=[pltpu.VM...  9.35 us
    pallas_call x1, Pallas kernels, encode(): pl.pallas_call(encode_kernel, out_shape=[jax.ShapeDtypeStruct((width, uni...  8.18 us

profile of v4, /device:TPU:0, one launch (start us, length us, event | category | flops | bytes accessed | tf_op | source)
XLA Modules:
  0.0 121.9 jit_solution(3545350638362919402)
XLA Ops:
  0.6 81.7 %front.1 = (bf16[512,1536]{1,0:T(8,128)(2,1)}, bf16[512,1536]{1,0:T(8,128)(2,1)}, bf16[512,1536]{1,0:T(8,128)(2,1)}, bf16[512,1536]{1,0:T(8,128)(2,1)}, bf16[64,1536]{1,0:T(8,128)(2,1)}, /*index=5*/f32[8,128]{1,0:T(8,128)}) custom-call(bf16[64,1536]{1,0:T(8,128)(2,1)} %refs_0_.1, bf16[64,1536]{1,0:T(8,128)(2,1)} %refs_1_.1, ...), custom_call_target="tpu_custom_call" | custom-call | tf_op jit(solution)/shard_map/front/pallas_call | solution.py:524
  82.4 22.0 %moments.1 = (bf16[1536,1536]{1,0:T(8,128)(2,1)}, bf16[1536,1536]{1,0:T(8,128)(2,1)}, bf16[1536,1536]{1,0:T(8,128)(2,1)S(1)}, bf16[1536,1536]{1,0:T(8,128)(2,1)S...) custom-call(f32[8,128]{1,0:T(8,128)} %get-tuple-element.36.factor_re, ...), custom_call_target="tpu_custom_call" | custom-call | tf_op jit(solution)/shard_map/moments/pallas_call | solution.py:714
  104.3 9.4 %tops.1 = (f32[8,4,1536]{2,1,0:T(4,128)S(1)}, f32[4,4,1536]{2,1,0:T(4,128)S(1)}) custom-call(f32[4,1536]{1,0:T(4,128)S(1)} %get-tuple-element.41.col_ref, f32[4,1536]{1,0:T(4,128)S(1)} %get-tuple-element.42.row_ref), custom_call_target="tpu_custom_call" | custom-call | tf_op jit(solution)/shard_map/tops/pallas_call | solution.py:781
  113.7 8.2 %encode.1 = (bf16[1536,1536]{1,0:T(8,128)(2,1)}, bf16[1536,1536]{1,0:T(8,128)(2,1)}, bf16[1536,1536]{1,0:T(8,128)(2,1)}, bf16[1536,1536]{1,0:T(8,128)(2,1)}, f32...) custom-call(f32[8,4,1536]{2,1,0:T(4,128)S(1)} %get-tuple-element.43., ...), custom_call_target="tpu_custom_call" | custom-call | tf_op jit(solution)/shard_map/encode/pallas_call | solution.py:882
